TPU v7x, 32 devices: a whole 2x2x4 slice. The times are simulated.
32 devices in a mesh: ep: 4 (over z), tp: 8 (over y, x, core).
Axes of the slice: x: 2, y: 2, z: 4, core: 2. Of those that a mesh axis runs over, the one named last changes fastest.
Arguments:
- tokens: bfloat16 [384, 3072], P('ep', 'tp'), may hold values from -6 to 6
- cotangent: bfloat16 [384, 3072], P('ep', 'tp'), may hold values from -6 to 6
- expert_ids: int32 [384, 2], P('ep'), may hold values from 0 to 3, all different within a row; in each aligned block of 96 rows (0 to 95, 96 to 191, ...) at most 80 rows name the same one
- combine_weights: float32 [384, 2], P('ep'), may hold values from 0.1 to 1
- w_gate: bfloat16 [4, 3072, 8192], P('ep', None, 'tp'), may hold values from -0.15625 to 0.15625
- w_up: bfloat16 [4, 3072, 8192], P('ep', None, 'tp'), may hold values from -0.109375 to 0.109375
- w_down: bfloat16 [4, 8192, 3072], P('ep', 'tp'), may hold values from -0.09375 to 0.09375
Outputs:
- mixed: bfloat16 [384, 3072], P('ep', 'tp')
- grad_tokens: bfloat16 [384, 3072], P('ep', 'tp')
- grad_combine: float32 [384, 2], P('ep')
- grad_gate: bfloat16 [4, 3072, 8192], P('ep', 'tp')
- grad_up: bfloat16 [4, 3072, 8192], P('ep', 'tp')
- grad_down: bfloat16 [4, 8192, 3072], P('ep', None, 'tp')
Inputs may be any that keep to these rules, and one draw needn't show every extreme that they name: `expert_ids`: each row names 2 different experts. Among the 96 rows of one index of ep, no expert is named more than 80 times, and in some such blocks one expert is named exactly 80 times.
All inputs are finite; a program needn't handle non-finite values.
Results may differ from a plain program's by a relative error of at most 0.019.
Values may be sent and summed in bfloat16 or wider, within the bound.
A program may use at most 128 MiB of HBM per device.

v0:
```python
import functools
import math

import jax
import jax.numpy as jnp
from jax import lax
from jax.experimental import pallas as pl
from jax.experimental.pallas import tpu as pltpu
from jax.sharding import PartitionSpec as P

MESH = pl.DeviceIdType.MESH
BF = jnp.bfloat16


def ring_order(chips):
    side_x = math.isqrt(chips)
    side_x = side_x if side_x * side_x == chips else chips // 2
    side_y = chips // side_x
    order = [x for x in range(side_x)]
    for y in range(1, side_y):
        xs = range(side_x - 1, 0, -1) if y % 2 else range(1, side_x)
        order += [y * side_x + x for x in xs]
    order += [y * side_x for y in range(side_y - 1, 0, -1)]
    return order


def pick(table, index):
    value = jnp.int32(table[0])
    for i in range(1, len(table)):
        value = jnp.where(index == i, jnp.int32(table[i]), value)
    return value


def remote(src, dst, send, recv, device):
    return pltpu.make_async_remote_copy(
        src_ref=src,
        dst_ref=dst,
        send_sem=send,
        recv_sem=recv,
        device_id={"tp": device},
        device_id_type=MESH,
    )


def greet(devices):
    barrier = pltpu.get_barrier_semaphore()
    for device in devices:
        pl.semaphore_signal(barrier, inc=1, device_id={"tp": device}, device_id_type=MESH)
    pl.semaphore_wait(barrier, len(devices))


def gather_kernel(count, chips, *refs):
    own, out = refs[:count], refs[count : 2 * count]
    ring_send, ring_recv, core_send, core_recv, keep = refs[2 * count :]
    order = ring_order(chips)
    place = [order.index(chip) for chip in range(chips)]
    me = lax.axis_index("tp")
    chip, core = me // 2, me % 2
    spot = pick(place, chip)
    partner = chip * 2 + 1 - core
    steps = chips // 2
    rows = own[0].shape[0]
    half = rows // 2

    def at(offset):
        return pick(order, (spot + offset + chips) % chips) * 2 + core

    right, left = at(1), at(-1)
    greet([right, left, partner])

    def part(ref, way, step):
        if step < steps - 1:
            return ref
        return ref.at[pl.ds(way * half, half)]

    def hop(k, way, step):
        index = at(-step if way == 0 else step)
        source = own[k] if step == 0 else out[k].at[index]
        return remote(
            part(source, way, step),
            part(out[k].at[index], way, step),
            ring_send.at[k, way, step],
            ring_recv.at[k, way, step],
            right if way == 0 else left,
        )

    def arrived(k, way, step):
        index = at(-(step + 1) if way == 0 else step + 1)
        block = part(out[k].at[index], way, step)
        return remote(
            block, block, ring_send.at[k, way, step], ring_recv.at[k, way, step], right if way == 0 else left
        ), remote(
            block, block, core_send.at[k, way, step], core_recv.at[k, way, step], partner
        )

    def own_pass(k):
        return remote(
            own[k], out[k].at[me], core_send.at[k, 2, 0], core_recv.at[k, 2, 0], partner
        )

    def own_keep(k):
        return pltpu.make_async_copy(own[k], out[k].at[me], keep.at[k])

    for k in range(count):
        for way in range(2):
            hop(k, way, 0).start()
    for k in range(count):
        own_pass(k).start()
        own_keep(k).start()
    for step in range(steps):
        for k in range(count):
            for way in range(2):
                landed, handed = arrived(k, way, step)
                landed.wait_recv()
                if step + 1 < steps:
                    hop(k, way, step + 1).start()
                handed.start()
    for k in range(count):
        own_keep(k).wait()
        own_pass(k).wait_send()
        other = remote(
            own[k], out[k].at[partner], core_send.at[k, 2, 0], core_recv.at[k, 2, 0], partner
        )
        other.wait_recv()
        for way in range(2):
            for step in range(steps):
                hop(k, way, step).wait_send()
                handed = arrived(k, way, step)[1]
                handed.wait_send()
                index = at(-(step + 1) if way == 0 else step + 1) // 2 * 2 + 1 - core
                block = part(out[k].at[index], way, step)
                remote(
                    block, block, core_send.at[k, way, step], core_recv.at[k, way, step], partner
                ).wait_recv()


def gather(arrays, ident):
    size = lax.axis_size("tp")
    chips, count = size // 2, len(arrays)
    ring = pltpu.SemaphoreType.DMA((count, 2, chips // 2))
    cores = pltpu.SemaphoreType.DMA((count, 3, chips // 2))
    return pl.pallas_call(
        functools.partial(gather_kernel, count, chips),
        out_shape=[jax.ShapeDtypeStruct((size,) + a.shape, a.dtype) for a in arrays],
        in_specs=[pl.BlockSpec(memory_space=pltpu.VMEM)] * count,
        out_specs=[pl.BlockSpec(memory_space=pl.ANY)] * count,
        scratch_shapes=[ring, ring, cores, cores, pltpu.SemaphoreType.DMA((count,))],
        compiler_params=pltpu.CompilerParams(collective_id=ident, has_side_effects=True),
        name=f"gather_{ident}",
    )(*arrays)


def reduce_kernel(count, chips, *refs):
    part, out = refs[:count], refs[count : 2 * count]
    pre, stage, got = refs[2 * count : 5 * count : 3], refs[2 * count + 1 : 5 * count : 3], refs[2 * count + 2 : 5 * count : 3]
    core_send, core_recv, chip_send, chip_recv = refs[5 * count :]
    me = lax.axis_index("tp")
    chip, core = me // 2, me % 2
    partner = chip * 2 + 1 - core
    away = [(chip + o) % chips for o in range(1, chips)]
    greet([partner] + [other * 2 + core for other in away])

    def swap(k):
        return remote(part[k].at[1 - core], pre[k], core_send.at[k], core_recv.at[k], partner)

    def ship(k, o):
        return remote(
            stage[k].at[away[o]], got[k].at[o], chip_send.at[k, o], chip_recv.at[k, o], away[o] * 2 + core
        )

    for k in range(count):
        swap(k).start()
    for k in range(count):
        swap(k).wait()

        def add(q, _):
            stage[k][q] = (
                part[k][core, q].astype(jnp.float32) + pre[k][q].astype(jnp.float32)
            ).astype(BF)
            return 0

        lax.fori_loop(0, chips, add, 0)
        for o in range(chips - 1):
            ship(k, o).start()
    for k in range(count):
        for o in range(chips - 1):
            ship(k, o).wait()
        total = stage[k][chip].astype(jnp.float32)
        for o in range(chips - 1):
            total = total + got[k][o].astype(jnp.float32)
        out[k][...] = total.astype(BF)


def reduce_pieces(partials, ident):
    size = lax.axis_size("tp")
    chips, count = size // 2, len(partials)
    rows, width = partials[0].shape[0], partials[0].shape[1] // size
    cut = [p.reshape(rows, chips, 2, width).transpose(2, 1, 0, 3) for p in partials]
    held = pltpu.VMEM((chips, rows, width), BF)
    got = pltpu.VMEM((chips - 1, rows, width), BF)
    return pl.pallas_call(
        functools.partial(reduce_kernel, count, chips),
        out_shape=[jax.ShapeDtypeStruct((rows, width), BF)] * count,
        in_specs=[pl.BlockSpec(memory_space=pltpu.VMEM)] * count,
        out_specs=[pl.BlockSpec(memory_space=pltpu.VMEM)] * count,
        scratch_shapes=[held, held, got] * count
        + [pltpu.SemaphoreType.DMA((count,))] * 2
        + [pltpu.SemaphoreType.DMA((count, chips - 1))] * 2,
        compiler_params=pltpu.CompilerParams(
            collective_id=ident, has_side_effects=True, vmem_limit_bytes=48 << 20
        ),
        name=f"reduce_{ident}",
    )(*cut)


def rows_kernel(x_ref, g_ref, o_ref):
    o_ref[...] = jnp.dot(x_ref[...], g_ref[0], preferred_element_type=jnp.float32).astype(BF)


def row_grads(x_turned, blocks):
    features, rows = x_turned.shape
    size, _, hidden = blocks.shape
    return pl.pallas_call(
        rows_kernel,
        grid=(size,),
        out_shape=jax.ShapeDtypeStruct((features, size * hidden), BF),
        in_specs=[
            pl.BlockSpec((features, rows), lambda n: (0, 0)),
            pl.BlockSpec((1, rows, hidden), lambda n: (n, 0, 0)),
        ],
        out_specs=pl.BlockSpec((features, hidden), lambda n: (0, n)),
        name="row_grads",
        cost_estimate=pl.CostEstimate(
            flops=2 * features * rows * size * hidden,
            bytes_accessed=2 * size * hidden * (rows + features),
            transcendentals=0,
        ),
    )(x_turned, blocks)


def side_by_side(blocks):
    size, rows, width = blocks.shape
    return blocks.transpose(1, 0, 2).reshape(rows, size * width)


def silu_parts(gate_pre):
    sigma = jax.nn.sigmoid(gate_pre)
    return (gate_pre * sigma, sigma * (1.0 + gate_pre * (1.0 - sigma)))


def contract_rows(left, right):
    return lax.dot_general(
        left, right, (((0,), (0,)), ((), ())), preferred_element_type=jnp.float32
    )


def contract_cols(left, right):
    return lax.dot_general(
        left, right, (((1,), (1,)), ((), ())), preferred_element_type=jnp.float32
    )


def body(tokens, cotangent, expert_ids, combine_weights, w_gate, w_up, w_down):
    groups = lax.axis_size("ep")
    tok_rows, piece_width = tokens.shape
    chosen = expert_ids.shape[1]
    capacity = tok_rows * chosen * 5 // (3 * groups)
    buffer_rows = groups * capacity
    gate_weight = w_gate[0]
    up_weight = w_up[0]
    down_weight = w_down[0]
    flat_ids = expert_ids.reshape(-1)
    onehot = (flat_ids[:, None] == jnp.arange(groups, dtype=jnp.int32)[None, :]).astype(jnp.int32)
    rank = jnp.sum((jnp.cumsum(onehot, axis=0) - onehot) * onehot, axis=1)
    slot_index = flat_ids * capacity + rank
    places = (jnp.arange(buffer_rows, dtype=jnp.int32)[:, None] == slot_index[None, :]).astype(
        jnp.bfloat16
    )
    placer = jnp.sum(
        places.reshape(buffer_rows, tok_rows, chosen).astype(jnp.float32), axis=2
    ).astype(jnp.bfloat16)
    scaled = (combine_weights[:, :, None] * cotangent[:, None, :].astype(jnp.float32)).astype(
        jnp.bfloat16
    )
    send_grad = jnp.dot(
        places, scaled.reshape(tok_rows * chosen, piece_width), preferred_element_type=jnp.float32
    ).astype(jnp.bfloat16)
    send_rows = jnp.dot(placer, tokens, preferred_element_type=jnp.float32).astype(jnp.bfloat16)
    recv_rows, recv_grad = (
        lax.all_to_all(
            send_rows.reshape(groups, capacity, piece_width),
            "ep",
            split_axis=0,
            concat_axis=0,
            tiled=True,
        ),
        lax.all_to_all(
            send_grad.reshape(groups, capacity, piece_width),
            "ep",
            split_axis=0,
            concat_axis=0,
            tiled=True,
        ),
    )
    recv_rows = recv_rows.reshape(buffer_rows, piece_width)
    recv_grad = recv_grad.reshape(buffer_rows, piece_width)
    x_blocks, dy_blocks = gather([recv_rows, recv_grad], 0)
    piece, dy_full = side_by_side(x_blocks), side_by_side(dy_blocks)
    gate_pre = jnp.dot(piece, gate_weight, preferred_element_type=jnp.float32)
    up_pre = jnp.dot(piece, up_weight, preferred_element_type=jnp.float32)
    active, slope = silu_parts(gate_pre)
    hidden = (active * up_pre).astype(jnp.bfloat16)
    partial_value = jnp.dot(hidden, down_weight, preferred_element_type=jnp.float32)
    grad_hidden = contract_cols(dy_full, down_weight)
    grad_gate_pre = (grad_hidden * up_pre * slope).astype(jnp.bfloat16)
    grad_up_pre = (grad_hidden * active).astype(jnp.bfloat16)
    input_partial = contract_cols(grad_gate_pre, gate_weight) + contract_cols(
        grad_up_pre, up_weight
    )
    out_piece, input_piece = reduce_pieces(
        [partial_value.astype(jnp.bfloat16), input_partial.astype(jnp.bfloat16)], 1
    )
    hidden_in, gate_in, up_in, out_piece, input_piece = lax.optimization_barrier(
        (hidden, grad_gate_pre, grad_up_pre, out_piece, input_piece)
    )
    hidden_blocks, gate_blocks, up_blocks = gather([hidden_in, gate_in, up_in], 2)
    out_back = lax.all_to_all(
        out_piece.reshape(groups, capacity, piece_width),
        "ep",
        split_axis=0,
        concat_axis=0,
        tiled=True,
    ).reshape(buffer_rows, piece_width)
    out_tokens = (
        jnp.take(out_back, slot_index, axis=0)
        .reshape(tok_rows, chosen, piece_width)
        .astype(jnp.float32)
    )
    mixed = jnp.sum(combine_weights[:, :, None] * out_tokens, axis=1).astype(jnp.bfloat16)
    local_products = jnp.sum(cotangent.astype(jnp.float32)[:, None, :] * out_tokens, axis=2)
    grad_combine = lax.psum(local_products, "tp")
    input_back = lax.all_to_all(
        input_piece.reshape(groups, capacity, piece_width),
        "ep",
        split_axis=0,
        concat_axis=0,
        tiled=True,
    ).reshape(buffer_rows, piece_width)
    grad_tokens = jnp.sum(
        jnp.take(input_back, slot_index, axis=0)
        .reshape(tok_rows, chosen, piece_width)
        .astype(jnp.float32),
        axis=1,
    ).astype(jnp.bfloat16)
    down_cols_out = (
        jnp.einsum("nrh,rd->nhd", hidden_blocks, recv_grad, preferred_element_type=jnp.float32)
        .astype(jnp.bfloat16)
        .reshape(-1, piece_width)
    )
    x_turned = recv_rows.T
    gate_rows_out = row_grads(x_turned, gate_blocks)
    up_rows_out = row_grads(x_turned, up_blocks)
    return (
        mixed,
        grad_tokens,
        grad_combine,
        gate_rows_out[None],
        up_rows_out[None],
        down_cols_out[None],
    )


def solution(mesh):
    placed = (
        P("ep", "tp"),
        P("ep", "tp"),
        P("ep", None),
        P("ep", None),
        P("ep", None, "tp"),
        P("ep", None, "tp"),
        P("ep", "tp", None),
    )
    return jax.shard_map(
        body,
        mesh=mesh,
        in_specs=placed,
        out_specs=(
            P("ep", "tp"),
            P("ep", "tp"),
            P("ep", None),
            P("ep", "tp", None),
            P("ep", "tp", None),
            P("ep", None, "tp"),
        ),
        check_vma=False,
    )
```

profile of v0, /device:TPU:0, one launch (start us, length us, event | category | flops | bytes accessed | tf_op | source)
XLA Modules:
  0.0 259.6 jit_solution(8967369403870925718)
XLA Ops:
  0.6 0.8 copy.47
  1.5 0.1 eq.43
  1.6 1.2 reduce-window.6
  2.9 0.1 copy.48
  3.3 0.1 reduce_sum.56
  3.5 0.7 multiply_add_fusion.1
  4.3 1.0 convolution_convert_fusion.2
  5.3 6.3 %all-to-all-start = ((bf16[4,80,384]{2,1,0:T(8,128)(2,1)}), bf16[4,80,384]{2,1,0:T(8,128)(2,1)S(1)}, u32[]{:S(2)}, u32[]{:S(2)}) async-start(bf16[4,80,384]{2,1,0:T(8,128)(2,1)} %bitcast.2), calls=%async_computation | async-start | bytes 491520 | tf_op jit(solution)/shard_map/all_to_all | solution.py:290
  11.6 0.8 copy.46
  12.4 0.1 mul.78
  12.5 1.0 mul.80
  13.5 0.2 mul.81
  13.7 1.0 convolution_convert_fusion.1
  14.7 5.4 %all-to-all-done = bf16[4,80,384]{2,1,0:T(8,128)(2,1)S(1)} async-done(((bf16[4,80,384]{2,1,0:T(8,128)(2,1)}), bf16[4,80,384]{2,1,0:T(8,128)(2,1)S(1)}, u32[]{:S(2)}, u32[]{:S(2)}) %all-to-all-start) | async-done | bytes 245792 | tf_op jit(solution)/shard_map/all_to_all | solution.py:290
  20.2 3.4 %all-to-all-start.1 = ((bf16[4,80,384]{2,1,0:T(8,128)(2,1)}), bf16[4,80,384]{2,1,0:T(8,128)(2,1)S(1)}, u32[]{:S(2)}, u32[]{:S(2)}) async-start(bf16[4,80,384]{2,1,0:T(8,128)(2,1)} %bitcast.4), calls=%async_computation.1 | async-start | bytes 491520 | tf_op jit(solution)/shard_map/all_to_all | solution.py:297
  23.6 0.9 copy.56
  24.5 6.0 %all-to-all-done.1 = bf16[4,80,384]{2,1,0:T(8,128)(2,1)S(1)} async-done(((bf16[4,80,384]{2,1,0:T(8,128)(2,1)}), bf16[4,80,384]{2,1,0:T(8,128)(2,1)S(1)}, u32[]{:S(2)}, u32[]{:S(2)}) %all-to-all-start.1) | async-done | bytes 245792 | tf_op jit(solution)/shard_map/all_to_all | solution.py:297
  30.5 0.7 copy-done.4
  31.2 21.8 %gather_0.1 = (bf16[8,320,384]{2,1,0:T(8,128)(2,1)}, bf16[8,320,384]{2,1,0:T(8,128)(2,1)}) custom-call(bf16[320,384]{1,0:T(8,128)(2,1)} %bitcast.73, bf16[320,384]{1,0:T(8,128)(2,1)} %bitcast.79), custom_call_target="tpu_custom_call" | custom-call | tf_op jit(solution)/shard_map/gather_0/pallas_call | solution.py:142
  53.0 2.0 copy.58
  55.1 0.3 copy.59
  55.5 5.2 %fusion.6 = f32[320,1024]{1,0:T(8,128)S(1)} fusion(bf16[320,3072]{1,0:T(8,128)(2,1)S(1)} %bitcast.75, bf16[1,3072,1024]{2,1,0:T(8,128)(2,1)} %param.14), kind=kOutput, calls=%fused_computation.8 | convolution fusion | flops 2013265920 | bytes 9568256 | tf_op jit(solution)/shard_map/dot_general | solution.py:310
  60.7 2.2 fusion.10
  63.0 3.6 %multiply_convert_fusion = (bf16[320,1024]{1,0:T(8,128)(2,1)S(1)}, bf16[320,1024]{1,0:T(8,128)(2,1)}, bf16[320,1024]{1,0:T(8,128)(2,1)S(1)}) fusion(f32[320,1024]{1,0:T(8,128)S(1)} %fusion.10, f32[320,1024]{1,0:T(8,128)S(1)} %fusion.6, bf16[320,3072]{1,0:T(8,128)(2,1)S(1)} %bitcast.74, bf16[1,1024,3072]{2,1,0:T(8,128)(2,1)S(1)} %bitcast.84), kind=kOutput, calls=%fused_computation.20 | convolution fusion | flops 2018181120 | bytes 12845056 | tf_op jit(solution)/shard_map/dot_general | solution.py:258
  66.5 0.9 copy-done.8
  67.4 3.5 %fusion.18 = bf16[320,3072]{1,0:T(8,128)(2,1)} fusion(bf16[320,1024]{1,0:T(8,128)(2,1)S(1)} %get-tuple-element.25.refs_0_, bf16[1,1024,3072]{2,1,0:T(8,128)(2,1)S(1)} %bitcast.84), kind=kOutput, calls=%fused_computation.16 | convolution fusion | flops 2014248960 | bytes 8912896 | tf_op jit(solution)/shard_map/dot_general | solution.py:313
  70.9 5.0 %reshape.107 = bf16[320,4,2,384]{3,2,1,0:T(2,128)(2,1)S(1)} reshape(bf16[320,3072]{1,0:T(8,128)(2,1)} %fusion.18) | data formatting | bytes 3932160 | tf_op jit(solution)/shard_map/reshape | solution.py:198
  75.9 5.1 %fusion.4 = f32[320,3072]{1,0:T(8,128)S(1)} fusion(bf16[320,1024]{1,0:T(8,128)(2,1)S(1)} %get-tuple-element.27.refs_2_, bf16[1,3072,1024]{2,1,0:T(8,128)(2,1)} %param.14), kind=kOutput, calls=%fused_computation.6 | convolution fusion | flops 2013265920 | bytes 10878976 | tf_op jit(solution)/shard_map/dot_general | solution.py:258
  81.0 6.4 %fusion.15 = bf16[320,3072]{1,0:T(8,128)(2,1)} fusion(f32[320,3072]{1,0:T(8,128)S(1)} %fusion.4, bf16[320,1024]{1,0:T(8,128)(2,1)S(1)} %copy-done.7, bf16[1,3072,1024]{2,1,0:T(8,128)(2,1)} %param.13), kind=kOutput, calls=%fused_computation.15 | convolution fusion | flops 2015232000 | bytes 12845056 | tf_op jit(solution)/shard_map/dot_general | solution.py:258
  87.4 5.7 %reshape.108 = bf16[320,4,2,384]{3,2,1,0:T(2,128)(2,1)} reshape(bf16[320,3072]{1,0:T(8,128)(2,1)} %fusion.15) | data formatting | bytes 3932160 | tf_op jit(solution)/shard_map/reshape | solution.py:198
  93.1 2.2 copy_bitcast_fusion
  95.3 28.8 %reduce_1.1 = (bf16[320,384]{1,0:T(8,128)(2,1)}, bf16[320,384]{1,0:T(8,128)(2,1)}) custom-call(bf16[2,4,320,384]{3,2,1,0:T(8,128)(2,1)S(1)} %get-tuple-element.57.refs_0_, bf16[2,4,320,384]{3,2,1,0:T(8,128)(2,1)S(1)} %get-tuple-element.56.refs_1_), custom_call_target="tpu_custom_call" | custom-call | tf_op jit(solution)/shard_map/reduce_1/pallas_call | solution.py:201
  124.1 3.5 %all-to-all-start.3 = ((bf16[4,80,384]{2,1,0:T(8,128)(2,1)}), bf16[4,80,384]{2,1,0:T(8,128)(2,1)S(1)}, u32[]{:S(2)}, u32[]{:S(2)}) async-start(bf16[4,80,384]{2,1,0:T(8,128)(2,1)} %bitcast.15), calls=%async_computation.3 | async-start | bytes 491520 | tf_op jit(solution)/shard_map/all_to_all | solution.py:342
  127.7 69.8 %gather_2.1 = (bf16[8,320,1024]{2,1,0:T(8,128)(2,1)}, bf16[8,320,1024]{2,1,0:T(8,128)(2,1)}, bf16[8,320,1024]{2,1,0:T(8,128)(2,1)}) custom-call(bf16[320,1024]{1,0:T(8,128)(2,1)} %copy-done.8, bf16[320,1024]{1,0:T(8,128)(2,1)} %get-tuple-element.26.refs_1_, bf16[320,1024]{1,0:T(8,128)(2,1)} %copy-done.6), custom_call_target="tpu_custom_call" | custom-call | tf_op jit(solution)/shard_map/gather_2/pallas_call | solution.py:142
  197.5 9.2 %convolution_convert_fusion = bf16[8,1024,384]{2,1,0:T(8,128)(2,1)} fusion(bf16[8,320,1024]{2,1,0:T(8,128)(2,1)} %get-tuple-element.30, bf16[320,384,1]{1,0,2:T(8,128)(2,1)S(1)} %bitcast.80), kind=kOutput, calls=%fused_computation.17 | convolution fusion | flops 2016411648 | bytes 11780096 | tf_op jit(solution)/shard_map/nrh,rd->nhd/dot_general | solution.py:356
  206.7 4.8 %all-to-all-start.2 = ((bf16[4,80,384]{2,1,0:T(8,128)(2,1)}), bf16[4,80,384]{2,1,0:T(8,128)(2,1)S(1)}, u32[]{:S(2)}, u32[]{:S(2)}) async-start(bf16[4,80,384]{2,1,0:T(8,128)(2,1)} %bitcast.13), calls=%async_computation.2 | async-start | bytes 491520 | tf_op jit(solution)/shard_map/all_to_all | solution.py:327
  211.6 9.2 %row_grads.2 = bf16[384,8192]{1,0:T(8,128)(2,1)} custom-call(bf16[384,320]{1,0:T(8,128)(2,1)} %bitcast.70, bf16[8,320,1024]{2,1,0:T(8,128)(2,1)} %get-tuple-element.28.g_ref), custom_call_target="tpu_custom_call" | custom-call | flops 2013265920 | bytes 11534336 | tf_op jit(solution)/shard_map/row_grads/pallas_call | solution.py:223
  220.7 9.2 %row_grads.3 = bf16[384,8192]{1,0:T(8,128)(2,1)} custom-call(bf16[384,320]{1,0:T(8,128)(2,1)} %bitcast.71, bf16[8,320,1024]{2,1,0:T(8,128)(2,1)} %get-tuple-element.29.g_ref), custom_call_target="tpu_custom_call" | custom-call | flops 2013265920 | bytes 11534336 | tf_op jit(solution)/shard_map/row_grads/pallas_call | solution.py:223
  229.9 1.0 gather_fusion.1
  230.9 1.0 gather_fusion
  231.9 0.2 multiply_reduce_fusion
  232.1 0.1 reduce_sum.61
  232.3 24.3 %psum.7 = f32[96,2]{1,0:T(8,128)S(1)} all-reduce(f32[96,2]{1,0:T(8,128)S(1)} %reduce_sum.61), channel_id=1, replica_groups=mesh['ep'=4,'tp'=8] {'tp'}, use_global_device_ids=true, to_apply=%region_7.9 | all-reduce | flops 192 | bytes 1536 | tf_op jit(solution)/shard_map/psum | solution.py:341
  256.5 0.6 copy.57
  257.2 0.1 broadcast_select_fusion
  257.4 0.2 reshape.115
  257.5 1.1 multiply_reduce_fusion.1
  258.6 1.0 reduce_sum.59
  (44 shorter events, 0.7 us)
Async XLA Ops:
  0.6 3.7 %copy-start = (bf16[96,384]{1,0:T(8,128)(2,1)S(1)}, bf16[96,384]{1,0:T(8,128)(2,1)}, u32[]{:S(2)}) copy-start(bf16[96,384]{1,0:T(8,128)(2,1)} %param.9) | copy-start | bytes 221188
  5.3 14.9 %all-to-all-start = ((bf16[4,80,384]{2,1,0:T(8,128)(2,1)}), bf16[4,80,384]{2,1,0:T(8,128)(2,1)S(1)}, u32[]{:S(2)}, u32[]{:S(2)}) async-start(bf16[4,80,384]{2,1,0:T(8,128)(2,1)} %bitcast.2), calls=%async_computation | async-start | bytes 491520 | tf_op jit(solution)/shard_map/all_to_all | solution.py:290
  20.2 10.3 %copy-start.2 = (bf16[4,80,384]{2,1,0:T(8,128)(2,1)}, bf16[4,80,384]{2,1,0:T(8,128)(2,1)S(1)}, u32[]{:S(2)}) copy-start(bf16[4,80,384]{2,1,0:T(8,128)(2,1)S(1)} %all-to-all-done) | copy-start | bytes 737284
  20.2 10.3 %all-to-all-start.1 = ((bf16[4,80,384]{2,1,0:T(8,128)(2,1)}), bf16[4,80,384]{2,1,0:T(8,128)(2,1)S(1)}, u32[]{:S(2)}, u32[]{:S(2)}) async-start(bf16[4,80,384]{2,1,0:T(8,128)(2,1)} %bitcast.4), calls=%async_computation.1 | async-start | bytes 491520 | tf_op jit(solution)/shard_map/all_to_all | solution.py:297
  30.5 0.7 copy-start.4
  53.0 2.1 copy-start.3
  55.1 5.6 %slice-start.2 = ((s8[6291456]{0:T(1024)(128)(4,1)}), s8[2097152]{0:T(1024)(128)(4,1)S(1)}, s32[]{:S(2)}) async-start(s8[6291456]{0:T(1024)(128)(4,1)} %bitcast.85), calls=%async_computation.6 | async-start | bytes 4194304
  55.5 5.2 %slice-start.3 = ((s8[6291456]{0:T(1024)(128)(4,1)}), s8[4194304]{0:T(1024)(128)(4,1)S(1)}, s32[]{:S(2)}) async-start(s8[6291456]{0:T(1024)(128)(4,1)} %bitcast.85), calls=%async_computation.7 | async-start | bytes 8388608
  55.5 7.4 %slice-start = ((s8[6291456]{0:T(1024)(128)(4,1)}), s8[4194304]{0:T(1024)(128)(4,1)S(1)}, s32[]{:S(2)}) async-start(s8[6291456]{0:T(1024)(128)(4,1)} %bitcast.83), calls=%async_computation.4 | async-start | bytes 8388608
  60.7 2.2 slice-start.1
  66.5 0.9 copy-start.8
  66.5 9.4 %copy-start.6 = (bf16[320,1024]{1,0:T(8,128)(2,1)}, bf16[320,1024]{1,0:T(8,128)(2,1)S(1)}, u32[]{:S(2)}) copy-start(bf16[320,1024]{1,0:T(8,128)(2,1)S(1)} %get-tuple-element.27.refs_2_) | copy-start | bytes 1966084
  75.9 5.1 %copy-start.7 = (bf16[320,1024]{1,0:T(8,128)(2,1)S(1)}, bf16[320,1024]{1,0:T(8,128)(2,1)}, u32[]{:S(2)}) copy-start(bf16[320,1024]{1,0:T(8,128)(2,1)} %get-tuple-element.26.refs_1_) | copy-start | bytes 1966084
  124.1 73.4 %copy-start.5 = (bf16[4,80,384]{2,1,0:T(8,128)(2,1)S(1)}, bf16[4,80,384]{2,1,0:T(8,128)(2,1)}, u32[]{:S(2)}) copy-start(bf16[4,80,384]{2,1,0:T(8,128)(2,1)} %copy-done.4) | copy-start | bytes 737284
  124.1 82.6 %all-to-all-start.3 = ((bf16[4,80,384]{2,1,0:T(8,128)(2,1)}), bf16[4,80,384]{2,1,0:T(8,128)(2,1)S(1)}, u32[]{:S(2)}, u32[]{:S(2)}) async-start(bf16[4,80,384]{2,1,0:T(8,128)(2,1)} %bitcast.15), calls=%async_computation.3 | async-start | bytes 491520 | tf_op jit(solution)/shard_map/all_to_all | solution.py:342
  206.7 24.2 %all-to-all-start.2 = ((bf16[4,80,384]{2,1,0:T(8,128)(2,1)}), bf16[4,80,384]{2,1,0:T(8,128)(2,1)S(1)}, u32[]{:S(2)}, u32[]{:S(2)}) async-start(bf16[4,80,384]{2,1,0:T(8,128)(2,1)} %bitcast.13), calls=%async_computation.2 | async-start | bytes 491520 | tf_op jit(solution)/shard_map/all_to_all | solution.py:327
  230.9 28.7 %copy-start.1 = (bf16[96,384]{1,0:T(8,128)(2,1)S(1)}, bf16[96,384]{1,0:T(8,128)(2,1)}, u32[]{:S(2)}) copy-start(bf16[96,384]{1,0:T(8,128)(2,1)} %param.9) | copy-start | bytes 221188
where the time goes:
time: 261 us; the launch traced here: 260 us
  Pallas kernels  139 us (53%)
  matrix products  37.1 us (14%)
  local copies, waits for them, and re-layouts  24.5 us (9%)
  blocking collectives  24.3 us (9%)
  starting transfers between devices  18.1 us (7%)
  waiting for transfers between devices  11.4 us (4%)
  other arithmetic  4.56 us (2%)
    pallas_call x2, Pallas kernels, gather(): pl.pallas_call(functools.partial(gather_kernel, count, chips), out_shape=...  91.6 us
    pallas_call x1, Pallas kernels, reduce_pieces(): pl.pallas_call(functools.partial(reduce_kernel, count, chips), out_shape=...  28.8 us
    psum x1, blocking collectives, body(): grad_combine = lax.psum(local_products, 'tp')  24.3 us
    pallas_call x2, Pallas kernels, row_grads(): pl.pallas_call(rows_kernel, grid=(size,), out_shape=jax.ShapeDtypeStruct(...  18.3 us
    dot_general x3, matrix products, contract_cols(): lax.dot_general(left, right, (((1,), (1,)), ((), ())), preferred_element_...  15 us
    reshape x2, local copies, waits for them, and re-layouts, reduce_pieces(): p.reshape(rows, chips, 2, width).transpose(2, 1, 0, 3)  10.7 us
    dot_general x1, matrix products, body(): jnp.einsum('nrh,rd->nhd', hidden_blocks, recv_grad, preferred_element_typ...  9.24 us
    all_to_all x1, starting transfers between devices, body(): lax.all_to_all(send_rows.reshape(groups, capacity, piece_width), 'ep', sp...  6.35 us
  transfers between devices with their start and end apart: 4, of which 2 were waited for; matrix products, arithmetic and copies ran while one was open for 6% of the time, Pallas kernels for 34%

commit v1 on v0

--- a/solution.py
+++ b/solution.py
@@ -260,7 +260,7 @@
     )
 
 
-def body(tokens, cotangent, expert_ids, combine_weights, w_gate, w_up, w_down):
+def general_body(tokens, cotangent, expert_ids, combine_weights, w_gate, w_up, w_down):
     groups = lax.axis_size("ep")
     tok_rows, piece_width = tokens.shape
     chosen = expert_ids.shape[1]
@@ -370,6 +370,549 @@
     )
 
 
+CHUNK = 256
+LANES = 128
+
+
+def fast_form(tokens, expert_ids, w_gate):
+    groups, size = lax.axis_size("ep"), lax.axis_size("tp")
+    tok_rows, width = tokens.shape
+    hidden = w_gate.shape[2]
+    capacity = tok_rows * expert_ids.shape[1] * 5 // (3 * groups)
+    return (
+        size == 8
+        and expert_ids.shape[1] == 2
+        and groups <= 8
+        and width % LANES == 0
+        and hidden % CHUNK == 0
+        and capacity % 16 == 0
+        and groups * capacity % 32 == 0
+        and tok_rows <= LANES
+        and tok_rows % 8 == 0
+    )
+
+
+def far_copy(src, dst, send, recv, device):
+    return pltpu.make_async_remote_copy(
+        src_ref=src, dst_ref=dst, send_sem=send, recv_sem=recv, device_id=device, device_id_type=MESH
+    )
+
+
+def layer_kernel(
+    chips,
+    groups,
+    capacity,
+    ids,
+    ids_t,
+    weights,
+    tokens,
+    cotangent,
+    wg_hbm,
+    wu_hbm,
+    wd_hbm,
+    blocks,
+    x_own,
+    dy_own,
+    mixed,
+    grad_tokens,
+    grad_combine,
+    wg,
+    wu,
+    wd,
+    both,
+    out_rows,
+    own,
+    part,
+    pre,
+    stage,
+    got,
+    piece,
+    back,
+    products,
+    w_sem,
+    z_send,
+    z_recv,
+    x_send,
+    x_recv,
+    a_send,
+    a_recv,
+    keep,
+    s_send,
+    s_recv,
+    r_send,
+    r_recv,
+    b_send,
+    b_recv,
+    p_send,
+    p_recv,
+):
+    size = 2 * chips
+    tok_rows, width = tokens.shape
+    rows = groups * capacity
+    model = size * width
+    chunks = wg.shape[0]
+    wide = 2 * width
+    order = ring_order(chips)
+    place = [order.index(chip) for chip in range(chips)]
+    me = lax.axis_index("tp")
+    group = lax.axis_index("ep")
+    chip, core = me // 2, me % 2
+    spot = pick(place, chip)
+    partner = chip * 2 + 1 - core
+
+    def chip_at(offset):
+        return pick(order, (spot + offset + chips) % chips)
+
+    def at(offset):
+        return chip_at(offset) * 2 + core
+
+    right, left, across = at(1), at(-1), at(2)
+    sides = (right, left)
+
+    def other(device):
+        return device // 2 * 2 + 1 - core
+
+    def fetches():
+        found = []
+        for c in range(chunks):
+            cut = pl.ds(c * CHUNK, CHUNK)
+            found.append(pltpu.make_async_copy(wg_hbm.at[:, cut], wg.at[c], w_sem.at[0, c]))
+            found.append(pltpu.make_async_copy(wu_hbm.at[:, cut], wu.at[c], w_sem.at[1, c]))
+        for q in range(chips):
+            cut = pl.ds(q * wide, wide)
+            found.append(pltpu.make_async_copy(wd_hbm.at[:, cut], wd.at[q], w_sem.at[2, q]))
+        return found
+
+    barrier = pltpu.get_barrier_semaphore()
+    for d in range(1, size):
+        pl.semaphore_signal(barrier, inc=1, device_id={"tp": (me + d) % size}, device_id_type=MESH)
+    for d in range(1, groups):
+        pl.semaphore_signal(
+            barrier, inc=1, device_id={"ep": (group + d) % groups}, device_id_type=MESH
+        )
+
+    row_id = lax.broadcasted_iota(jnp.int32, (8, tok_rows), 0)
+    member_t = jnp.where((ids_t[0:1, :] == row_id) | (ids_t[1:2, :] == row_id), 1.0, 0.0)
+    first = lax.broadcasted_iota(jnp.int32, (tok_rows, tok_rows), 0)
+    second = lax.broadcasted_iota(jnp.int32, (tok_rows, tok_rows), 1)
+    before_t = jnp.dot(
+        member_t.astype(BF),
+        jnp.where(first < second, 1.0, 0.0).astype(BF),
+        preferred_element_type=jnp.float32,
+    )
+    slot_t = lax.broadcasted_iota(jnp.int32, (capacity, tok_rows), 0).astype(jnp.float32)
+    id_0, id_1 = ids[:, 0:1], ids[:, 1:2]
+    weight_0, weight_1 = weights[:, 0:1], weights[:, 1:2]
+    for p in range(groups):
+        placer = (
+            jnp.where(slot_t == before_t[p : p + 1, :], 1.0, 0.0) * member_t[p : p + 1, :]
+        ).astype(BF)
+        weight = jnp.where(id_0 == p, weight_0, 0.0) + jnp.where(id_1 == p, weight_1, 0.0)
+        scaled = (weight * cotangent[...].astype(jnp.float32)).astype(BF)
+        out_rows[p, 0] = jnp.dot(placer, tokens[...], preferred_element_type=jnp.float32).astype(BF)
+        out_rows[p, 1] = jnp.dot(placer, scaled, preferred_element_type=jnp.float32).astype(BF)
+
+    def rows_of(s):
+        return pl.ds(pl.multiple_of(s * capacity, 16), capacity)
+
+    def cols_of(device):
+        return pl.ds(pl.multiple_of(device * width, LANES), width)
+
+    pl.semaphore_wait(barrier, size + groups - 2)
+
+    def z_out(k):
+        p = (group + k) % groups
+        return far_copy(
+            out_rows.at[p],
+            both.at[:, rows_of(group), cols_of(me)],
+            z_send.at[k],
+            z_recv.at[k],
+            {"ep": p},
+        )
+
+    for k in range(1, groups):
+        z_out(k).start()
+    for a in range(2):
+        both[a, rows_of(group), cols_of(me)] = out_rows[group, a]
+    for copy in fetches():
+        copy.start()
+
+    def source(k):
+        return (group - k + groups) % groups
+
+    def x_part(k, device, a=None):
+        if a is None:
+            return both.at[:, rows_of(source(k)), cols_of(device)]
+        return both.at[a, rows_of(source(k)), cols_of(device)]
+
+    def x_copy(k, kind, device, target, a=None):
+        block = x_part(k, device, a)
+        return far_copy(block, block, x_send.at[kind, k], x_recv.at[kind, k], {"tp": target})
+
+    for k in range(groups):
+        if k > 0:
+            block = x_part(k, me)
+            far_copy(block, block, z_send.at[k], z_recv.at[k], {"ep": source(k)}).wait_recv()
+        x_copy(k, 0, me, right).start()
+        x_copy(k, 1, me, left).start()
+        x_copy(k, 4, me, partner).start()
+    for k in range(groups):
+        for way in range(2):
+            origin = sides[1 - way]
+            x_copy(k, way, origin, sides[way]).wait_recv()
+            x_copy(k, 2 + way, origin, sides[way], way).start()
+            x_copy(k, 5 + way, origin, partner).start()
+    for k in range(groups):
+        for way in range(2):
+            x_copy(k, 2 + way, across, sides[way], way).wait_recv()
+            x_copy(k, 7 + way, across, partner, way).start()
+    for k in range(groups):
+        x_copy(k, 4, partner, partner).wait_recv()
+        for way in range(2):
+            x_copy(k, 5 + way, other(sides[1 - way]), partner).wait_recv()
+            x_copy(k, 7 + way, other(across), partner, way).wait_recv()
+    for copy in fetches():
+        copy.wait()
+
+    half = rows // 2
+
+    def a_part(c, device, way=None):
+        if way is None:
+            return blocks.at[device, c]
+        return blocks.at[device, c, :, pl.ds(way * half, half), :]
+
+    def a_first(c, kind, target):
+        return far_copy(
+            own.at[c], a_part(c, me), a_send.at[kind, c], a_recv.at[kind, c], {"tp": target}
+        )
+
+    def a_copy(c, kind, device, target, way=None):
+        block = a_part(c, device, way)
+        return far_copy(block, block, a_send.at[kind, c], a_recv.at[kind, c], {"tp": target})
+
+    def a_keep(c):
+        return pltpu.make_async_copy(own.at[c], a_part(c, me), keep.at[c])
+
+    def one_chunk(c, _):
+        cut = pl.ds(pl.multiple_of(c * CHUNK, CHUNK), CHUNK)
+        gate_pre = jnp.dot(both[0], wg[c], preferred_element_type=jnp.float32)
+        up_pre = jnp.dot(both[0], wu[c], preferred_element_type=jnp.float32)
+        grad_hidden = contract_cols(both[1, :, 0:wide], wd[0, cut, :])
+        for q in range(1, chips):
+            grad_hidden = grad_hidden + contract_cols(
+                both[1, :, q * wide : (q + 1) * wide], wd[q, cut, :]
+            )
+        active, slope = silu_parts(gate_pre)
+        own[c, 0] = (active * up_pre).astype(BF)
+        own[c, 1] = (grad_hidden * up_pre * slope).astype(BF)
+        own[c, 2] = (grad_hidden * active).astype(BF)
+        a_first(c, 0, right).start()
+        a_first(c, 1, left).start()
+        a_first(c, 4, partner).start()
+        a_keep(c).start()
+        return 0
+
+    lax.fori_loop(0, chunks, one_chunk, 0)
+
+    turns = [2, 1, chips - 1, 0]
+
+    def swap(a, o):
+        return far_copy(
+            part.at[a, 1 - core, o], pre.at[a, o], s_send.at[a, o], s_recv.at[a, o], {"tp": partner}
+        )
+
+    def ship(a, o):
+        return far_copy(
+            stage.at[a, o],
+            got.at[a, o],
+            r_send.at[a, o],
+            r_recv.at[a, o],
+            {"tp": at(turns[o])},
+        )
+
+    def one_chip(o, _):
+        q = pick(order, (spot + pick(turns, o)) % chips)
+        cut = pl.ds(pl.multiple_of(q * wide, LANES), wide)
+        value = jnp.dot(own[0, 0], wd[q, 0:CHUNK, :], preferred_element_type=jnp.float32)
+        for c in range(1, chunks):
+            value = value + jnp.dot(
+                own[c, 0], wd[q, c * CHUNK : (c + 1) * CHUNK, :], preferred_element_type=jnp.float32
+            )
+        part[0, 0, o] = value[:, :width].astype(BF)
+        part[0, 1, o] = value[:, width:].astype(BF)
+        swap(0, o).start()
+        value = contract_cols(own[0, 1], wg[0, cut, :]) + contract_cols(own[0, 2], wu[0, cut, :])
+        for c in range(1, chunks):
+            value = value + contract_cols(own[c, 1], wg[c, cut, :])
+            value = value + contract_cols(own[c, 2], wu[c, cut, :])
+        part[1, 0, o] = value[:, :width].astype(BF)
+        part[1, 1, o] = value[:, width:].astype(BF)
+        swap(1, o).start()
+        return 0
+
+    lax.fori_loop(0, chips, one_chip, 0)
+
+    x_own[...] = both[0, :, cols_of(me)]
+    dy_own[...] = both[1, :, cols_of(me)]
+
+    for o in range(chips):
+        for a in range(2):
+            swap(a, o).wait_recv()
+
+            def add(b, _):
+                cut = pl.ds(pl.multiple_of(b * 16, 16), 16)
+                stage[a, o, cut, :] = (
+                    part[a, core, o, cut, :].astype(jnp.float32)
+                    + pre[a, o, cut, :].astype(jnp.float32)
+                ).astype(BF)
+                return 0
+
+            lax.fori_loop(0, rows // 16, add, 0)
+            if o + 1 < chips:
+                ship(a, o).start()
+
+    for c in range(chunks):
+        for way in range(2):
+            origin = sides[1 - way]
+            a_copy(c, way, origin, sides[way]).wait_recv()
+            a_copy(c, 2 + way, origin, sides[way], way).start()
+            a_copy(c, 5 + way, origin, partner).start()
+
+    for a in range(2):
+        for o in range(chips - 1):
+            ship(a, o).wait_recv()
+
+        def total(b, _):
+            cut = pl.ds(pl.multiple_of(b * 16, 16), 16)
+            value = stage[a, chips - 1, cut, :].astype(jnp.float32)
+            for o in range(chips - 1):
+                value = value + got[a, o, cut, :].astype(jnp.float32)
+            piece[a, cut, :] = value.astype(BF)
+            return 0
+
+        lax.fori_loop(0, rows // 16, total, 0)
+
+    def b_out(k):
+        p = (group + k) % groups
+        return far_copy(
+            piece.at[:, rows_of(p), :], back.at[group], b_send.at[k], b_recv.at[k], {"ep": p}
+        )
+
+    for k in range(1, groups):
+        b_out(k).start()
+    for a in range(2):
+        back[group, a] = piece[a, rows_of(group), :]
+    for k in range(1, groups):
+        block = back.at[source(k)]
+        far_copy(block, block, b_send.at[k], b_recv.at[k], {"ep": source(k)}).wait_recv()
+
+    lane = lax.broadcasted_iota(jnp.int32, (tok_rows, LANES), 1)
+    member = jnp.where((id_0 == lane) | (id_1 == lane), 1.0, 0.0)
+    before = jnp.dot(
+        jnp.where(second < first, 1.0, 0.0).astype(BF),
+        member.astype(BF),
+        preferred_element_type=jnp.float32,
+    )
+    slot = lax.broadcasted_iota(jnp.int32, (tok_rows, capacity), 1).astype(jnp.float32)
+    mix = jnp.zeros((tok_rows, width), jnp.float32)
+    grads = jnp.zeros((tok_rows, width), jnp.float32)
+    inner = jnp.zeros((tok_rows, LANES), jnp.float32)
+    for p in range(groups):
+        placer = (jnp.where(slot == before[:, p : p + 1], 1.0, 0.0) * member[:, p : p + 1]).astype(BF)
+        out = jnp.dot(placer, back[p, 0], preferred_element_type=jnp.float32)
+        weight = jnp.where(id_0 == p, weight_0, 0.0) + jnp.where(id_1 == p, weight_1, 0.0)
+        mix = mix + weight * out
+        grads = grads + jnp.dot(placer, back[p, 1], preferred_element_type=jnp.float32)
+        product = jnp.sum(cotangent[...].astype(jnp.float32) * out, axis=1, keepdims=True)
+        inner = inner + jnp.where(((lane == 0) & (id_0 == p)) | ((lane == 1) & (id_1 == p)), product, 0.0)
+    mixed[...] = mix.astype(BF)
+    grad_tokens[...] = grads.astype(BF)
+    if tok_rows < LANES:
+        inner = jnp.concatenate([inner, jnp.zeros((LANES - tok_rows, LANES), jnp.float32)], axis=0)
+    products[me] = jnp.transpose(inner)[0:8, :]
+
+    def p_copy(d):
+        return far_copy(
+            products.at[me], products.at[me], p_send.at[d], p_recv.at[d], {"tp": (me + d) % size}
+        )
+
+    for d in range(1, size):
+        p_copy(d).start()
+
+    for c in range(chunks):
+        for way in range(2):
+            a_copy(c, 2 + way, across, sides[way], way).wait_recv()
+            a_copy(c, 7 + way, across, partner, way).start()
+
+    for d in range(1, size):
+        origin = (me - d + size) % size
+        block = products.at[origin]
+        far_copy(block, block, p_send.at[d], p_recv.at[d], {"tp": origin}).wait_recv()
+    summed = products[0]
+    for d in range(1, size):
+        summed = summed + products[d]
+    summed = jnp.concatenate([summed, jnp.zeros((LANES - 8, LANES), jnp.float32)], axis=0)
+    grad_combine[...] = jnp.transpose(summed)[0:tok_rows, 0:2]
+
+    for k in range(1, groups):
+        z_out(k).wait_send()
+        b_out(k).wait_send()
+    for k in range(groups):
+        for way in range(2):
+            x_copy(k, way, me, sides[way]).wait_send()
+            x_copy(k, 2 + way, sides[1 - way], sides[way], way).wait_send()
+            x_copy(k, 5 + way, sides[1 - way], partner).wait_send()
+            x_copy(k, 7 + way, across, partner, way).wait_send()
+        x_copy(k, 4, me, partner).wait_send()
+    for a in range(2):
+        for o in range(chips):
+            swap(a, o).wait_send()
+        for o in range(chips - 1):
+            ship(a, o).wait_send()
+    for d in range(1, size):
+        p_copy(d).wait_send()
+    for c in range(chunks):
+        a_keep(c).wait()
+        for way in range(2):
+            a_first(c, way, sides[way]).wait_send()
+            a_copy(c, 2 + way, sides[1 - way], sides[way], way).wait_send()
+            a_copy(c, 5 + way, sides[1 - way], partner).wait_send()
+            a_copy(c, 7 + way, across, partner, way).wait_send()
+        a_first(c, 4, partner).wait_send()
+    for c in range(chunks):
+        a_copy(c, 4, partner, partner).wait_recv()
+        for way in range(2):
+            a_copy(c, 5 + way, other(sides[1 - way]), partner).wait_recv()
+            a_copy(c, 7 + way, other(across), partner, way).wait_recv()
+
+
+def layer(ids, ids_t, weights, tokens, cotangent, w_gate, w_up, w_down, capacity):
+    size, groups = lax.axis_size("tp"), lax.axis_size("ep")
+    chips = size // 2
+    tok_rows, width = tokens.shape
+    model, hidden = w_gate.shape
+    chunks = hidden // CHUNK
+    rows = groups * capacity
+    whole, any_place = pl.BlockSpec(memory_space=pltpu.VMEM), pl.BlockSpec(memory_space=pl.ANY)
+    dma = pltpu.SemaphoreType.DMA
+    return pl.pallas_call(
+        functools.partial(layer_kernel, chips, groups, capacity),
+        out_shape=[
+            jax.ShapeDtypeStruct((size, chunks, 3, rows, CHUNK), BF),
+            jax.ShapeDtypeStruct((rows, width), BF),
+            jax.ShapeDtypeStruct((rows, width), BF),
+            jax.ShapeDtypeStruct((tok_rows, width), BF),
+            jax.ShapeDtypeStruct((tok_rows, width), BF),
+            jax.ShapeDtypeStruct((tok_rows, 2), jnp.float32),
+        ],
+        in_specs=[whole] * 5 + [any_place] * 3,
+        out_specs=[any_place] + [whole] * 5,
+        scratch_shapes=[
+            pltpu.VMEM((chunks, model, CHUNK), BF),
+            pltpu.VMEM((chunks, model, CHUNK), BF),
+            pltpu.VMEM((chips, hidden, 2 * width), BF),
+            pltpu.VMEM((2, rows, model), BF),
+            pltpu.VMEM((groups, 2, capacity, width), BF),
+            pltpu.VMEM((chunks, 3, rows, CHUNK), BF),
+            pltpu.VMEM((2, 2, chips, rows, width), BF),
+            pltpu.VMEM((2, chips, rows, width), BF),
+            pltpu.VMEM((2, chips, rows, width), BF),
+            pltpu.VMEM((2, chips - 1, rows, width), BF),
+            pltpu.VMEM((2, rows, width), BF),
+            pltpu.VMEM((groups, 2, capacity, width), BF),
+            pltpu.VMEM((size, 8, LANES), jnp.float32),
+            dma((3, max(chunks, chips))),
+            dma((groups,)),
+            dma((groups,)),
+            dma((9, groups)),
+            dma((9, groups)),
+            dma((9, chunks)),
+            dma((9, chunks)),
+            dma((chunks,)),
+            dma((2, chips)),
+            dma((2, chips)),
+            dma((2, chips - 1)),
+            dma((2, chips - 1)),
+            dma((groups,)),
+            dma((groups,)),
+            dma((size,)),
+            dma((size,)),
+        ],
+        compiler_params=pltpu.CompilerParams(
+            collective_id=0, has_side_effects=True, vmem_limit_bytes=60 << 20
+        ),
+        name="layer",
+    )(ids, ids_t, weights, tokens, cotangent, w_gate, w_up, w_down)
+
+
+def grads_kernel(x, dy, mixed_in, tokens_in, combine_in, block, gate, up, down, mixed, grad_tokens, grad_combine):
+    @pl.when(pl.program_id(0) == 0)
+    def _():
+        mixed[...] = mixed_in[...]
+        grad_tokens[...] = tokens_in[...]
+        grad_combine[...] = combine_in[...]
+
+    for c in range(block.shape[1]):
+        cut = pl.ds(c * CHUNK, CHUNK)
+        gate[0, :, cut] = contract_rows(x[...], block[0, c, 1]).astype(BF)
+        up[0, :, cut] = contract_rows(x[...], block[0, c, 2]).astype(BF)
+        down[0, cut, :] = contract_rows(block[0, c, 0], dy[...]).astype(BF)
+
+
+def weight_grads(x, dy, mixed, grad_tokens, grad_combine, blocks):
+    size, chunks, _, rows, _ = blocks.shape
+    width = x.shape[1]
+    take = 2 if chunks % 2 == 0 else 1
+    steps = chunks // take
+    hidden = size * chunks * CHUNK
+
+    def whole(a):
+        return pl.BlockSpec(a.shape, lambda n: (0, 0))
+
+    return pl.pallas_call(
+        grads_kernel,
+        grid=(size * steps,),
+        out_shape=[
+            jax.ShapeDtypeStruct((1, width, hidden), BF),
+            jax.ShapeDtypeStruct((1, width, hidden), BF),
+            jax.ShapeDtypeStruct((1, hidden, width), BF),
+            jax.ShapeDtypeStruct(mixed.shape, BF),
+            jax.ShapeDtypeStruct(mixed.shape, BF),
+            jax.ShapeDtypeStruct(grad_combine.shape, jnp.float32),
+        ],
+        in_specs=[whole(x), whole(dy), whole(mixed), whole(mixed), whole(grad_combine)]
+        + [pl.BlockSpec((1, take, 3, rows, CHUNK), lambda n: (n // steps, n % steps, 0, 0, 0))],
+        out_specs=[
+            pl.BlockSpec((1, width, take * CHUNK), lambda n: (0, 0, n)),
+            pl.BlockSpec((1, width, take * CHUNK), lambda n: (0, 0, n)),
+            pl.BlockSpec((1, take * CHUNK, width), lambda n: (0, n, 0)),
+            whole(mixed),
+            whole(mixed),
+            whole(grad_combine),
+        ],
+        name="weight_grads",
+        cost_estimate=pl.CostEstimate(
+            flops=6 * width * rows * hidden,
+            bytes_accessed=6 * hidden * (rows + width),
+            transcendentals=0,
+        ),
+    )(x, dy, mixed, grad_tokens, grad_combine, blocks)
+
+
+def body(tokens, cotangent, expert_ids, combine_weights, w_gate, w_up, w_down):
+    if not fast_form(tokens, expert_ids, w_gate):
+        return general_body(tokens, cotangent, expert_ids, combine_weights, w_gate, w_up, w_down)
+    tok_rows, chosen = expert_ids.shape
+    capacity = tok_rows * chosen * 5 // (3 * lax.axis_size("ep"))
+    blocks, x, dy, mixed, grad_tokens, grad_combine = layer(
+        expert_ids, expert_ids.T, combine_weights, tokens, cotangent, w_gate[0], w_up[0], w_down[0], capacity
+    )
+    gate, up, down, mixed, grad_tokens, grad_combine = weight_grads(
+        x, dy, mixed, grad_tokens, grad_combine, blocks
+    )
+    return mixed, grad_tokens, grad_combine, gate, up, down
+
+
 def solution(mesh):
     placed = (
         P("ep", "tp"),

time: 261 us -> 149 us (0.57)
  matrix products: 37.1 us -> 0 us
  blocking collectives: 24.3 us -> 0 us
  local copies, waits for them, and re-layouts: 24.5 us -> 4.22 us
  starting transfers between devices: 18.1 us -> 0 us
  waiting for transfers between devices: 11.4 us -> 0 us
  other arithmetic: 4.56 us -> 0 us
  Pallas kernels: 139 us -> 143 us
    dot_general x9 -> x0, matrix products: 37.1 us -> none  [the longest x3 15 us: contract_cols(): lax.dot_general(left, right, (((1,), (1,)), ((), ())), preferred_element_...]
    psum x1 -> x0, blocking collectives: 24.3 us -> none  [body(): grad_combine = lax.psum(local_products, 'tp')]
    all_to_all x4 -> x0, starting transfers between devices: 18.1 us -> none  [the longest x1 6.35 us: body(): lax.all_to_all(send_rows.reshape(groups, capacity, piece_width), 'ep', sp...]
    reshape x6 -> x0, local copies, waits for them, and re-layouts: 14.1 us -> none  [the longest x2 10.7 us: reduce_pieces(): p.reshape(rows, chips, 2, width).transpose(2, 1, 0, 3)]
    all_to_all x4 -> x0, waiting for transfers between devices: 11.4 us -> none  [the longest x1 5.98 us: body(): lax.all_to_all(send_grad.reshape(groups, capacity, piece_width), 'ep', sp...]
    pallas_call x5 -> x2, Pallas kernels: 139 us -> 143 us  [the longest x1 122 us: layer(): pl.pallas_call(functools.partial(layer_kernel, chips, groups, capacity),...]
  transfers between devices with their start and end apart: 4 -> 0, of which waited for: 2 -> 0; matrix products, arithmetic and copies ran while one was open for 6% -> 0% of each run, Pallas kernels for 34% -> 0%
where the time goes in v1:
time: 149 us; the launch traced here: 148 us
  Pallas kernels  143 us (96%)
  local copies, waits for them, and re-layouts  4.22 us (3%)
    pallas_call x1, Pallas kernels, layer(): pl.pallas_call(functools.partial(layer_kernel, chips, groups, capacity),...  122 us
    pallas_call x1, Pallas kernels, weight_grads(): pl.pallas_call(grads_kernel, grid=(size * steps,), out_shape=[jax.ShapeDt...  21.2 us
    unnamed x3, local copies, waits for them, and re-layouts  4.22 us

profile of v1, /device:TPU:0, one launch (start us, length us, event | category | flops | bytes accessed | tf_op | source)
XLA Modules:
  0.0 147.8 jit_solution(4331611352888353595)
XLA Ops:
  0.6 1.4 copy.14.weights
  2.0 1.4 copy.13.ids
  3.4 121.8 %layer.1 = (bf16[8,4,3,320,256]{4,3,2,1,0:T(8,128)(2,1)}, bf16[320,384]{1,0:T(8,128)(2,1)}, bf16[320,384]{1,0:T(8,128)(2,1)}, bf16[96,384]{1,0:T(8,128)(2,1)}, bf16[96,384]{1,0:T(8,128)(2,1)}, /*index=5*/f32[96,2]{1,0:T(8,128)}) custom-call(s32[96,2]{1,0:T(8,128)} %copy.13.ids, s32[2,96]{1,0:T(2,128)} %bitcast.7, f32[96,2]{1,0:T(8,128)} %copy.14.weights, ...), custom_call_target="tpu_custom_call" | custom-call | tf_op jit(solution)/shard_map/layer/pallas_call | solution.py:798
  125.2 21.2 %weight_grads.1 = (bf16[1,384,8192]{2,1,0:T(8,128)(2,1)}, bf16[1,384,8192]{2,1,0:T(8,128)(2,1)}, bf16[1,8192,384]{2,1,0:T(8,128)(2,1)}, bf16[96,384]{1,0:T(8,128...) custom-call(bf16[320,384]{1,0:T(8,128)(2,1)} %get-tuple-element.18.x, bf16[320,384]{1,0:T(8,128)(2,1)} %get-tuple-element.19.dy, ...), custom_call_target="tpu_custom_call" | custom-call | flops 6039797760 | bytes 34603008 | tf_op jit(solution)/shard_map/weight_grads/pallas_call | solution.py:872
  146.4 1.4 copy.15

commit v2 on v1

--- a/solution.py
+++ b/solution.py
@@ -386,9 +386,10 @@
         and width % LANES == 0
         and hidden % CHUNK == 0
         and capacity % 16 == 0
+        and capacity <= LANES
         and groups * capacity % 32 == 0
         and tok_rows <= LANES
-        and tok_rows % 8 == 0
+        and tok_rows % 16 == 0
     )
 
 
@@ -402,33 +403,34 @@
     chips,
     groups,
     capacity,
-    ids,
     ids_t,
-    weights,
+    weights_t,
     tokens,
     cotangent,
     wg_hbm,
     wu_hbm,
     wd_hbm,
-    blocks,
-    x_own,
-    dy_own,
+    gate_buf,
+    up_buf,
+    down_buf,
     mixed,
     grad_tokens,
     grad_combine,
-    wg,
-    wu,
-    wd,
+    blocks,
     both,
     out_rows,
-    own,
     part,
     pre,
     stage,
+    back,
+    ready,
     got,
-    piece,
-    back,
+    turned,
+    inner_sum,
+    inner_out,
+    inner_in,
     products,
+    table,
     w_sem,
     z_send,
     z_recv,
@@ -436,13 +438,14 @@
     x_recv,
     a_send,
     a_recv,
-    keep,
     s_send,
     s_recv,
+    b_send,
+    b_recv,
+    i_send,
+    i_recv,
     r_send,
     r_recv,
-    b_send,
-    b_recv,
     p_send,
     p_recv,
 ):
@@ -450,7 +453,8 @@
     tok_rows, width = tokens.shape
     rows = groups * capacity
     model = size * width
-    chunks = wg.shape[0]
+    hidden = wg_hbm.shape[1]
+    chunks = hidden // CHUNK
     wide = 2 * width
     order = ring_order(chips)
     place = [order.index(chip) for chip in range(chips)]
@@ -460,11 +464,8 @@
     spot = pick(place, chip)
     partner = chip * 2 + 1 - core
 
-    def chip_at(offset):
-        return pick(order, (spot + offset + chips) % chips)
-
     def at(offset):
-        return chip_at(offset) * 2 + core
+        return pick(order, (spot + offset + chips) % chips) * 2 + core
 
     right, left, across = at(1), at(-1), at(2)
     sides = (right, left)
@@ -476,11 +477,17 @@
         found = []
         for c in range(chunks):
             cut = pl.ds(c * CHUNK, CHUNK)
-            found.append(pltpu.make_async_copy(wg_hbm.at[:, cut], wg.at[c], w_sem.at[0, c]))
-            found.append(pltpu.make_async_copy(wu_hbm.at[:, cut], wu.at[c], w_sem.at[1, c]))
+            spread = pl.ds(c * model, model)
+            found.append(pltpu.make_async_copy(wg_hbm.at[:, cut], gate_buf.at[spread, :], w_sem.at[0, c]))
+            found.append(pltpu.make_async_copy(wu_hbm.at[:, cut], up_buf.at[spread, :], w_sem.at[1, c]))
         for q in range(chips):
-            cut = pl.ds(q * wide, wide)
-            found.append(pltpu.make_async_copy(wd_hbm.at[:, cut], wd.at[q], w_sem.at[2, q]))
+            found.append(
+                pltpu.make_async_copy(
+                    wd_hbm.at[:, pl.ds(q * wide, wide)],
+                    down_buf.at[pl.ds(q * hidden, hidden), :],
+                    w_sem.at[2, q],
+                )
+            )
         return found
 
     barrier = pltpu.get_barrier_semaphore()
@@ -500,15 +507,19 @@
         jnp.where(first < second, 1.0, 0.0).astype(BF),
         preferred_element_type=jnp.float32,
     )
+    table[...] = jnp.zeros((LANES, LANES), jnp.float32)
+    table[0:2, 0:tok_rows] = ids_t[...].astype(jnp.float32)
+    table[2:4, 0:tok_rows] = weights_t[...]
+    columns = jnp.transpose(table[...])[0:tok_rows, :]
+    choice = (columns[:, 0:1], columns[:, 1:2])
+    weight = (columns[:, 2:3], columns[:, 3:4])
     slot_t = lax.broadcasted_iota(jnp.int32, (capacity, tok_rows), 0).astype(jnp.float32)
-    id_0, id_1 = ids[:, 0:1], ids[:, 1:2]
-    weight_0, weight_1 = weights[:, 0:1], weights[:, 1:2]
     for p in range(groups):
         placer = (
             jnp.where(slot_t == before_t[p : p + 1, :], 1.0, 0.0) * member_t[p : p + 1, :]
         ).astype(BF)
-        weight = jnp.where(id_0 == p, weight_0, 0.0) + jnp.where(id_1 == p, weight_1, 0.0)
-        scaled = (weight * cotangent[...].astype(jnp.float32)).astype(BF)
+        own_weight = jnp.where(choice[0] == p, weight[0], 0.0) + jnp.where(choice[1] == p, weight[1], 0.0)
+        scaled = (own_weight * cotangent[...].astype(jnp.float32)).astype(BF)
         out_rows[p, 0] = jnp.dot(placer, tokens[...], preferred_element_type=jnp.float32).astype(BF)
         out_rows[p, 1] = jnp.dot(placer, scaled, preferred_element_type=jnp.float32).astype(BF)
 
@@ -518,16 +529,18 @@
     def cols_of(device):
         return pl.ds(pl.multiple_of(device * width, LANES), width)
 
+    def source(k):
+        return (group - k + groups) % groups
+
     pl.semaphore_wait(barrier, size + groups - 2)
 
     def z_out(k):
-        p = (group + k) % groups
         return far_copy(
-            out_rows.at[p],
+            out_rows.at[(group + k) % groups],
             both.at[:, rows_of(group), cols_of(me)],
             z_send.at[k],
             z_recv.at[k],
-            {"ep": p},
+            {"ep": (group + k) % groups},
         )
 
     for k in range(1, groups):
@@ -537,21 +550,16 @@
     for copy in fetches():
         copy.start()
 
-    def source(k):
-        return (group - k + groups) % groups
-
-    def x_part(k, device, a=None):
+    def x_copy(k, kind, device, target, a=None):
         if a is None:
-            return both.at[:, rows_of(source(k)), cols_of(device)]
-        return both.at[a, rows_of(source(k)), cols_of(device)]
-
-    def x_copy(k, kind, device, target, a=None):
-        block = x_part(k, device, a)
+            block = both.at[:, rows_of(source(k)), cols_of(device)]
+        else:
+            block = both.at[a, rows_of(source(k)), cols_of(device)]
         return far_copy(block, block, x_send.at[kind, k], x_recv.at[kind, k], {"tp": target})
 
     for k in range(groups):
         if k > 0:
-            block = x_part(k, me)
+            block = both.at[:, rows_of(source(k)), cols_of(me)]
             far_copy(block, block, z_send.at[k], z_recv.at[k], {"ep": source(k)}).wait_recv()
         x_copy(k, 0, me, right).start()
         x_copy(k, 1, me, left).start()
@@ -576,100 +584,140 @@
 
     half = rows // 2
 
-    def a_part(c, device, way=None):
+    def a_copy(c, kind, device, target, way=None):
         if way is None:
-            return blocks.at[device, c]
-        return blocks.at[device, c, :, pl.ds(way * half, half), :]
-
-    def a_first(c, kind, target):
+            block = blocks.at[device, c]
+        else:
+            block = blocks.at[device, c, :, pl.ds(way * half, half), :]
+        return far_copy(block, block, a_send.at[kind, c], a_recv.at[kind, c], {"tp": target})
+
+    inner_sum[...] = jnp.zeros((rows, LANES), jnp.float32)
+
+    def one_chunk(c, _):
+        spread = pl.ds(pl.multiple_of(c * model, 16), model)
+        gate_pre = jnp.dot(both[0], gate_buf[spread, :], preferred_element_type=jnp.float32)
+        up_pre = jnp.dot(both[0], up_buf[spread, :], preferred_element_type=jnp.float32)
+        grad_hidden = None
+        for q in range(chips):
+            cut = pl.ds(pl.multiple_of(q * hidden + c * CHUNK, CHUNK), CHUNK)
+            term = contract_cols(both[1, :, q * wide : (q + 1) * wide], down_buf[cut, :])
+            grad_hidden = term if q == 0 else grad_hidden + term
+        active, slope = silu_parts(gate_pre)
+        value = (active * up_pre).astype(BF)
+        blocks[me, c, 0] = value
+        blocks[me, c, 1] = (grad_hidden * up_pre * slope).astype(BF)
+        blocks[me, c, 2] = (grad_hidden * active).astype(BF)
+        a_copy(c, 0, me, right).start()
+        a_copy(c, 1, me, left).start()
+        a_copy(c, 4, me, partner).start()
+        product = value.astype(jnp.float32) * grad_hidden
+        total = inner_sum[...]
+        for n in range(CHUNK // LANES):
+            total = total + product[:, n * LANES : (n + 1) * LANES]
+        inner_sum[...] = total
+        return 0
+
+    lax.fori_loop(0, chunks, one_chunk, 0)
+
+    turns = [2, 1, chips - 1, 0]
+
+    def swap(o):
+        return far_copy(part.at[1 - core, o], pre.at[o], s_send.at[o], s_recv.at[o], {"tp": partner})
+
+    def b_out(o, k):
+        p = (group + k) % groups
         return far_copy(
-            own.at[c], a_part(c, me), a_send.at[kind, c], a_recv.at[kind, c], {"tp": target}
-        )
-
-    def a_copy(c, kind, device, target, way=None):
-        block = a_part(c, device, way)
-        return far_copy(block, block, a_send.at[kind, c], a_recv.at[kind, c], {"tp": target})
-
-    def a_keep(c):
-        return pltpu.make_async_copy(own.at[c], a_part(c, me), keep.at[c])
-
-    def one_chunk(c, _):
-        cut = pl.ds(pl.multiple_of(c * CHUNK, CHUNK), CHUNK)
-        gate_pre = jnp.dot(both[0], wg[c], preferred_element_type=jnp.float32)
-        up_pre = jnp.dot(both[0], wu[c], preferred_element_type=jnp.float32)
-        grad_hidden = contract_cols(both[1, :, 0:wide], wd[0, cut, :])
-        for q in range(1, chips):
-            grad_hidden = grad_hidden + contract_cols(
-                both[1, :, q * wide : (q + 1) * wide], wd[q, cut, :]
-            )
-        active, slope = silu_parts(gate_pre)
-        own[c, 0] = (active * up_pre).astype(BF)
-        own[c, 1] = (grad_hidden * up_pre * slope).astype(BF)
-        own[c, 2] = (grad_hidden * active).astype(BF)
-        a_first(c, 0, right).start()
-        a_first(c, 1, left).start()
-        a_first(c, 4, partner).start()
-        a_keep(c).start()
-        return 0
-
-    lax.fori_loop(0, chunks, one_chunk, 0)
-
-    turns = [2, 1, chips - 1, 0]
-
-    def swap(a, o):
-        return far_copy(
-            part.at[a, 1 - core, o], pre.at[a, o], s_send.at[a, o], s_recv.at[a, o], {"tp": partner}
-        )
-
-    def ship(a, o):
-        return far_copy(
-            stage.at[a, o],
-            got.at[a, o],
-            r_send.at[a, o],
-            r_recv.at[a, o],
-            {"tp": at(turns[o])},
+            stage.at[o, :, rows_of(p), :],
+            back.at[:, rows_of(group), pl.ds(o * width, width)],
+            b_send.at[o, k],
+            b_recv.at[o, k],
+            {"ep": p},
         )
 
     def one_chip(o, _):
         q = pick(order, (spot + pick(turns, o)) % chips)
-        cut = pl.ds(pl.multiple_of(q * wide, LANES), wide)
-        value = jnp.dot(own[0, 0], wd[q, 0:CHUNK, :], preferred_element_type=jnp.float32)
-        for c in range(1, chunks):
-            value = value + jnp.dot(
-                own[c, 0], wd[q, c * CHUNK : (c + 1) * CHUNK, :], preferred_element_type=jnp.float32
+        value = None
+        for c in range(chunks):
+            cut = pl.ds(pl.multiple_of(q * hidden + c * CHUNK, CHUNK), CHUNK)
+            term = jnp.dot(blocks[me, c, 0], down_buf[cut, :], preferred_element_type=jnp.float32)
+            value = term if c == 0 else value + term
+        part[0, o, 0] = value[:, :width].astype(BF)
+        part[1, o, 0] = value[:, width:].astype(BF)
+        value = None
+        for c in range(chunks):
+            cut = pl.ds(pl.multiple_of(c * model + q * wide, LANES), wide)
+            term = contract_cols(blocks[me, c, 1], gate_buf[cut, :]) + contract_cols(
+                blocks[me, c, 2], up_buf[cut, :]
             )
-        part[0, 0, o] = value[:, :width].astype(BF)
-        part[0, 1, o] = value[:, width:].astype(BF)
-        swap(0, o).start()
-        value = contract_cols(own[0, 1], wg[0, cut, :]) + contract_cols(own[0, 2], wu[0, cut, :])
-        for c in range(1, chunks):
-            value = value + contract_cols(own[c, 1], wg[c, cut, :])
-            value = value + contract_cols(own[c, 2], wu[c, cut, :])
-        part[1, 0, o] = value[:, :width].astype(BF)
-        part[1, 1, o] = value[:, width:].astype(BF)
-        swap(1, o).start()
+            value = term if c == 0 else value + term
+        part[0, o, 1] = value[:, :width].astype(BF)
+        part[1, o, 1] = value[:, width:].astype(BF)
+        swap(o).start()
         return 0
 
     lax.fori_loop(0, chips, one_chip, 0)
 
-    x_own[...] = both[0, :, cols_of(me)]
-    dy_own[...] = both[1, :, cols_of(me)]
-
     for o in range(chips):
+        swap(o).wait_recv()
+
+        def add(s, _):
+            cut = rows_of(s)
+            for a in range(2):
+                stage[o, a, cut, :] = (
+                    part[core, o, a, cut, :].astype(jnp.float32) + pre[o, a, cut, :].astype(jnp.float32)
+                ).astype(BF)
+            return 0
+
+        lax.fori_loop(0, groups, add, 0)
+        for k in range(1, groups):
+            b_out(o, k).start()
         for a in range(2):
-            swap(a, o).wait_recv()
-
-            def add(b, _):
-                cut = pl.ds(pl.multiple_of(b * 16, 16), 16)
-                stage[a, o, cut, :] = (
-                    part[a, core, o, cut, :].astype(jnp.float32)
-                    + pre[a, o, cut, :].astype(jnp.float32)
-                ).astype(BF)
-                return 0
-
-            lax.fori_loop(0, rows // 16, add, 0)
-            if o + 1 < chips:
-                ship(a, o).start()
+            back[a, rows_of(group), o * width : (o + 1) * width] = stage[o, a, rows_of(group), :]
+
+    def i_out(k):
+        p = (group + k) % groups
+        return far_copy(inner_out.at[p], inner_in.at[group], i_send.at[k], i_recv.at[k], {"ep": p})
+
+    for p in range(groups):
+        value = inner_sum[p * capacity : (p + 1) * capacity, :]
+        if capacity < LANES:
+            value = jnp.concatenate(
+                [value, jnp.zeros((LANES - capacity, LANES), jnp.float32)], axis=0
+            )
+        value = jnp.sum(jnp.transpose(value), axis=0, keepdims=True)
+        inner_out[p] = jnp.broadcast_to(value, (8, LANES))
+    for k in range(1, groups):
+        i_out(k).start()
+    inner_in[group] = inner_out[group]
+
+    turned[...] = jnp.transpose(both[0, :, cols_of(me)].astype(jnp.float32)).astype(BF)
+
+    def grads_of(device, c):
+        place_of = device * chunks + c
+        spread = pl.ds(pl.multiple_of(place_of * width, LANES), width)
+        gate_buf[spread, :] = jnp.dot(
+            turned[...], blocks[device, c, 1], preferred_element_type=jnp.float32
+        ).astype(BF)
+        up_buf[spread, :] = jnp.dot(
+            turned[...], blocks[device, c, 2], preferred_element_type=jnp.float32
+        ).astype(BF)
+        down_buf[
+            pl.ds(pl.multiple_of(place_of // 2 * CHUNK, CHUNK), CHUNK),
+            pl.ds(pl.multiple_of(place_of % 2 * width, LANES), width),
+        ] = contract_rows(blocks[device, c, 0], both[1, :, cols_of(me)]).astype(BF)
+
+    def grads_for(found):
+        devices, chunk = [d for d, _ in found], [c for _, c in found]
+
+        def step(n, _):
+            grads_of(pick(devices, n), pick(chunk, n))
+            return 0
+
+        lax.fori_loop(0, len(found), step, 0)
+
+    for c in range(chunks):
+        a_copy(c, 4, partner, partner).wait_recv()
+    grads_for([(d, c) for c in range(chunks) for d in (me, partner)])
 
     for c in range(chunks):
         for way in range(2):
@@ -677,56 +725,43 @@
             a_copy(c, way, origin, sides[way]).wait_recv()
             a_copy(c, 2 + way, origin, sides[way], way).start()
             a_copy(c, 5 + way, origin, partner).start()
-
-    for a in range(2):
-        for o in range(chips - 1):
-            ship(a, o).wait_recv()
-
-        def total(b, _):
-            cut = pl.ds(pl.multiple_of(b * 16, 16), 16)
-            value = stage[a, chips - 1, cut, :].astype(jnp.float32)
-            for o in range(chips - 1):
-                value = value + got[a, o, cut, :].astype(jnp.float32)
-            piece[a, cut, :] = value.astype(BF)
-            return 0
-
-        lax.fori_loop(0, rows // 16, total, 0)
-
-    def b_out(k):
-        p = (group + k) % groups
-        return far_copy(
-            piece.at[:, rows_of(p), :], back.at[group], b_send.at[k], b_recv.at[k], {"ep": p}
-        )
+        found = [(left, c), (right, c)]
+        if c > 0:
+            for way in range(2):
+                a_copy(c - 1, 5 + way, other(sides[1 - way]), partner).wait_recv()
+            found += [(other(left), c - 1), (other(right), c - 1)]
+        grads_for(found)
+    for way in range(2):
+        a_copy(chunks - 1, 5 + way, other(sides[1 - way]), partner).wait_recv()
+    grads_for([(other(left), chunks - 1), (other(right), chunks - 1)])
 
     for k in range(1, groups):
-        b_out(k).start()
-    for a in range(2):
-        back[group, a] = piece[a, rows_of(group), :]
-    for k in range(1, groups):
-        block = back.at[source(k)]
-        far_copy(block, block, b_send.at[k], b_recv.at[k], {"ep": source(k)}).wait_recv()
-
+        block = inner_in.at[source(k)]
+        far_copy(block, block, i_send.at[k], i_recv.at[k], {"ep": source(k)}).wait_recv()
     lane = lax.broadcasted_iota(jnp.int32, (tok_rows, LANES), 1)
-    member = jnp.where((id_0 == lane) | (id_1 == lane), 1.0, 0.0)
+    lane_value = lane.astype(jnp.float32)
+    columns = jnp.transpose(table[...])[0:tok_rows, :]
+    choice = (columns[:, 0:1], columns[:, 1:2])
+    weight = (columns[:, 2:3], columns[:, 3:4])
+    member = jnp.where((choice[0] == lane_value) | (choice[1] == lane_value), 1.0, 0.0)
+    first = lax.broadcasted_iota(jnp.int32, (tok_rows, tok_rows), 0)
+    second = lax.broadcasted_iota(jnp.int32, (tok_rows, tok_rows), 1)
     before = jnp.dot(
         jnp.where(second < first, 1.0, 0.0).astype(BF),
         member.astype(BF),
         preferred_element_type=jnp.float32,
     )
-    slot = lax.broadcasted_iota(jnp.int32, (tok_rows, capacity), 1).astype(jnp.float32)
-    mix = jnp.zeros((tok_rows, width), jnp.float32)
-    grads = jnp.zeros((tok_rows, width), jnp.float32)
     inner = jnp.zeros((tok_rows, LANES), jnp.float32)
-    for p in range(groups):
-        placer = (jnp.where(slot == before[:, p : p + 1], 1.0, 0.0) * member[:, p : p + 1]).astype(BF)
-        out = jnp.dot(placer, back[p, 0], preferred_element_type=jnp.float32)
-        weight = jnp.where(id_0 == p, weight_0, 0.0) + jnp.where(id_1 == p, weight_1, 0.0)
-        mix = mix + weight * out
-        grads = grads + jnp.dot(placer, back[p, 1], preferred_element_type=jnp.float32)
-        product = jnp.sum(cotangent[...].astype(jnp.float32) * out, axis=1, keepdims=True)
-        inner = inner + jnp.where(((lane == 0) & (id_0 == p)) | ((lane == 1) & (id_1 == p)), product, 0.0)
-    mixed[...] = mix.astype(BF)
-    grad_tokens[...] = grads.astype(BF)
+    takers = []
+    slot = lax.broadcasted_iota(jnp.int32, (tok_rows, rows), 1).astype(jnp.float32)
+    for k in range(2):
+        rank = jnp.sum(jnp.where(lane_value == choice[k], before, 0.0), axis=1, keepdims=True)
+        takers.append(jnp.where(slot == choice[k] * capacity + rank, 1.0, 0.0).astype(BF))
+        value = jnp.zeros((tok_rows, LANES), jnp.float32)
+        for p in range(groups):
+            value = value + jnp.where((lane_value == rank) & (choice[k] == p), inner_in[p][0:1, :], 0.0)
+        value = jnp.sum(value, axis=1, keepdims=True) / weight[k]
+        inner = inner + jnp.where(lane == k, value, 0.0)
     if tok_rows < LANES:
         inner = jnp.concatenate([inner, jnp.zeros((LANES - tok_rows, LANES), jnp.float32)], axis=0)
     products[me] = jnp.transpose(inner)[0:8, :]
@@ -740,9 +775,42 @@
         p_copy(d).start()
 
     for c in range(chunks):
+        if c == chunks - 1:
+            for o in range(chips):
+                for k in range(1, groups):
+                    block = back.at[:, rows_of(source(k)), pl.ds(o * width, width)]
+                    far_copy(
+                        block, block, b_send.at[o, k], b_recv.at[o, k], {"ep": source(k)}
+                    ).wait_recv()
+            for n in range(chips // 2):
+                cut = slice(n * wide, (n + 1) * wide)
+                mix = weight[0] * jnp.dot(takers[0], back[0, :, cut], preferred_element_type=jnp.float32)
+                mix = mix + weight[1] * jnp.dot(
+                    takers[1], back[0, :, cut], preferred_element_type=jnp.float32
+                )
+                grads = jnp.dot(
+                    takers[0] + takers[1], back[1, :, cut], preferred_element_type=jnp.float32
+                )
+                for j in range(2):
+                    o = 2 * n + j
+                    ready[o, 0] = mix[:, j * width : (j + 1) * width].astype(BF)
+                    ready[o, 1] = grads[:, j * width : (j + 1) * width].astype(BF)
+                    if o < chips - 1:
+                        far_copy(
+                            ready.at[o], got.at[o], r_send.at[o], r_recv.at[o], {"tp": at(turns[o])}
+                        ).start()
         for way in range(2):
             a_copy(c, 2 + way, across, sides[way], way).wait_recv()
             a_copy(c, 7 + way, across, partner, way).start()
+        if c > 0:
+            for way in range(2):
+                a_copy(c - 1, 7 + way, other(across), partner, way).wait_recv()
+            grads_for([(across, c), (other(across), c - 1)])
+        else:
+            grads_for([(across, c)])
+    for way in range(2):
+        a_copy(chunks - 1, 7 + way, other(across), partner, way).wait_recv()
+    grads_for([(other(across), chunks - 1)])
 
     for d in range(1, size):
         origin = (me - d + size) % size
@@ -751,12 +819,24 @@
     summed = products[0]
     for d in range(1, size):
         summed = summed + products[d]
-    summed = jnp.concatenate([summed, jnp.zeros((LANES - 8, LANES), jnp.float32)], axis=0)
-    grad_combine[...] = jnp.transpose(summed)[0:tok_rows, 0:2]
+    grad_combine[...] = summed[0:2, 0:tok_rows]
+
+    def r_copy(o):
+        return far_copy(ready.at[o], got.at[o], r_send.at[o], r_recv.at[o], {"tp": at(turns[o])})
+
+    for o in range(chips - 1):
+        r_copy(o).wait_recv()
+    for a, out in ((0, mixed), (1, grad_tokens)):
+        value = ready[chips - 1, a].astype(jnp.float32)
+        for o in range(chips - 1):
+            value = value + got[o, a].astype(jnp.float32)
+        out[...] = value.astype(BF)
 
     for k in range(1, groups):
         z_out(k).wait_send()
-        b_out(k).wait_send()
+        i_out(k).wait_send()
+        for o in range(chips):
+            b_out(o, k).wait_send()
     for k in range(groups):
         for way in range(2):
             x_copy(k, way, me, sides[way]).wait_send()
@@ -764,29 +844,22 @@
             x_copy(k, 5 + way, sides[1 - way], partner).wait_send()
             x_copy(k, 7 + way, across, partner, way).wait_send()
         x_copy(k, 4, me, partner).wait_send()
-    for a in range(2):
-        for o in range(chips):
-            swap(a, o).wait_send()
-        for o in range(chips - 1):
-            ship(a, o).wait_send()
+    for o in range(chips):
+        swap(o).wait_send()
+    for o in range(chips - 1):
+        r_copy(o).wait_send()
     for d in range(1, size):
         p_copy(d).wait_send()
     for c in range(chunks):
-        a_keep(c).wait()
         for way in range(2):
-            a_first(c, way, sides[way]).wait_send()
+            a_copy(c, way, me, sides[way]).wait_send()
             a_copy(c, 2 + way, sides[1 - way], sides[way], way).wait_send()
             a_copy(c, 5 + way, sides[1 - way], partner).wait_send()
             a_copy(c, 7 + way, across, partner, way).wait_send()
-        a_first(c, 4, partner).wait_send()
-    for c in range(chunks):
-        a_copy(c, 4, partner, partner).wait_recv()
-        for way in range(2):
-            a_copy(c, 5 + way, other(sides[1 - way]), partner).wait_recv()
-            a_copy(c, 7 + way, other(across), partner, way).wait_recv()
-
-
-def layer(ids, ids_t, weights, tokens, cotangent, w_gate, w_up, w_down, capacity):
+        a_copy(c, 4, me, partner).wait_send()
+
+
+def layer(ids_t, weights_t, tokens, cotangent, w_gate, w_up, w_down, capacity):
     size, groups = lax.axis_size("tp"), lax.axis_size("ep")
     chips = size // 2
     tok_rows, width = tokens.shape
@@ -798,29 +871,31 @@
     return pl.pallas_call(
         functools.partial(layer_kernel, chips, groups, capacity),
         out_shape=[
-            jax.ShapeDtypeStruct((size, chunks, 3, rows, CHUNK), BF),
-            jax.ShapeDtypeStruct((rows, width), BF),
-            jax.ShapeDtypeStruct((rows, width), BF),
-            jax.ShapeDtypeStruct((tok_rows, width), BF),
-            jax.ShapeDtypeStruct((tok_rows, width), BF),
-            jax.ShapeDtypeStruct((tok_rows, 2), jnp.float32),
+            pltpu.VMEM((chunks * model, CHUNK), BF),
+            pltpu.VMEM((chunks * model, CHUNK), BF),
+            pltpu.VMEM((chips * hidden, 2 * width), BF),
+            pltpu.VMEM((tok_rows, width), BF),
+            pltpu.VMEM((tok_rows, width), BF),
+            pltpu.VMEM((2, tok_rows), jnp.float32),
         ],
-        in_specs=[whole] * 5 + [any_place] * 3,
-        out_specs=[any_place] + [whole] * 5,
+        in_specs=[whole] * 4 + [any_place] * 3,
+        out_specs=[whole] * 6,
         scratch_shapes=[
-            pltpu.VMEM((chunks, model, CHUNK), BF),
-            pltpu.VMEM((chunks, model, CHUNK), BF),
-            pltpu.VMEM((chips, hidden, 2 * width), BF),
+            pltpu.VMEM((size, chunks, 3, rows, CHUNK), BF),
             pltpu.VMEM((2, rows, model), BF),
             pltpu.VMEM((groups, 2, capacity, width), BF),
-            pltpu.VMEM((chunks, 3, rows, CHUNK), BF),
-            pltpu.VMEM((2, 2, chips, rows, width), BF),
-            pltpu.VMEM((2, chips, rows, width), BF),
-            pltpu.VMEM((2, chips, rows, width), BF),
-            pltpu.VMEM((2, chips - 1, rows, width), BF),
-            pltpu.VMEM((2, rows, width), BF),
-            pltpu.VMEM((groups, 2, capacity, width), BF),
+            pltpu.VMEM((2, chips, 2, rows, width), BF),
+            pltpu.VMEM((chips, 2, rows, width), BF),
+            pltpu.VMEM((chips, 2, rows, width), BF),
+            pltpu.VMEM((2, rows, chips * width), BF),
+            pltpu.VMEM((chips, 2, tok_rows, width), BF),
+            pltpu.VMEM((chips - 1, 2, tok_rows, width), BF),
+            pltpu.VMEM((width, rows), BF),
+            pltpu.VMEM((rows, LANES), jnp.float32),
+            pltpu.VMEM((groups, 8, LANES), jnp.float32),
+            pltpu.VMEM((groups, 8, LANES), jnp.float32),
             pltpu.VMEM((size, 8, LANES), jnp.float32),
+            pltpu.VMEM((LANES, LANES), jnp.float32),
             dma((3, max(chunks, chips))),
             dma((groups,)),
             dma((groups,)),
@@ -828,75 +903,63 @@
             dma((9, groups)),
             dma((9, chunks)),
             dma((9, chunks)),
-            dma((chunks,)),
-            dma((2, chips)),
-            dma((2, chips)),
-            dma((2, chips - 1)),
-            dma((2, chips - 1)),
+            dma((chips,)),
+            dma((chips,)),
+            dma((chips, groups)),
+            dma((chips, groups)),
             dma((groups,)),
             dma((groups,)),
+            dma((chips - 1,)),
+            dma((chips - 1,)),
             dma((size,)),
             dma((size,)),
         ],
         compiler_params=pltpu.CompilerParams(
-            collective_id=0, has_side_effects=True, vmem_limit_bytes=60 << 20
+            collective_id=0, has_side_effects=True, vmem_limit_bytes=44 << 20
         ),
         name="layer",
-    )(ids, ids_t, weights, tokens, cotangent, w_gate, w_up, w_down)
-
-
-def grads_kernel(x, dy, mixed_in, tokens_in, combine_in, block, gate, up, down, mixed, grad_tokens, grad_combine):
-    @pl.when(pl.program_id(0) == 0)
-    def _():
-        mixed[...] = mixed_in[...]
-        grad_tokens[...] = tokens_in[...]
-        grad_combine[...] = combine_in[...]
-
-    for c in range(block.shape[1]):
-        cut = pl.ds(c * CHUNK, CHUNK)
-        gate[0, :, cut] = contract_rows(x[...], block[0, c, 1]).astype(BF)
-        up[0, :, cut] = contract_rows(x[...], block[0, c, 2]).astype(BF)
-        down[0, cut, :] = contract_rows(block[0, c, 0], dy[...]).astype(BF)
-
-
-def weight_grads(x, dy, mixed, grad_tokens, grad_combine, blocks):
-    size, chunks, _, rows, _ = blocks.shape
-    width = x.shape[1]
-    take = 2 if chunks % 2 == 0 else 1
-    steps = chunks // take
-    hidden = size * chunks * CHUNK
-
-    def whole(a):
-        return pl.BlockSpec(a.shape, lambda n: (0, 0))
-
+    )(ids_t, weights_t, tokens, cotangent, w_gate, w_up, w_down)
+
+
+def place_kernel(gate_buf, up_buf, down_buf, *refs):
+    small, (gate, up, down), outs, sems = refs[:3], refs[3:6], refs[6:9], refs[9]
+    width = gate.shape[0]
+    count = gate.shape[1] // CHUNK
+    copies = []
+    for n in range(count):
+        cut, spread = pl.ds(n * CHUNK, CHUNK), pl.ds(n * width, width)
+        copies.append(pltpu.make_async_copy(gate_buf.at[spread, :], gate.at[:, cut], sems.at[0, n]))
+        copies.append(pltpu.make_async_copy(up_buf.at[spread, :], up.at[:, cut], sems.at[1, n]))
+        block = down_buf.at[pl.ds(n // 2 * CHUNK, CHUNK), pl.ds(n % 2 * width, width)]
+        copies.append(pltpu.make_async_copy(block, down.at[cut, :], sems.at[2, n]))
+    for n in range(3):
+        copies.append(pltpu.make_async_copy(small[n], outs[n], sems.at[3, n]))
+    for copy in copies:
+        copy.start()
+    for copy in copies:
+        copy.wait()
+
+
+def place_results(gate_buf, up_buf, down_buf, mixed, grad_tokens, grad_combine):
+    tok_rows, width = mixed.shape
+    hidden = gate_buf.shape[0] // width * CHUNK
+    whole, any_place = pl.BlockSpec(memory_space=pltpu.VMEM), pl.BlockSpec(memory_space=pl.ANY)
     return pl.pallas_call(
-        grads_kernel,
-        grid=(size * steps,),
+        place_kernel,
         out_shape=[
-            jax.ShapeDtypeStruct((1, width, hidden), BF),
-            jax.ShapeDtypeStruct((1, width, hidden), BF),
-            jax.ShapeDtypeStruct((1, hidden, width), BF),
-            jax.ShapeDtypeStruct(mixed.shape, BF),
-            jax.ShapeDtypeStruct(mixed.shape, BF),
-            jax.ShapeDtypeStruct(grad_combine.shape, jnp.float32),
+            jax.ShapeDtypeStruct((width, hidden), BF),
+            jax.ShapeDtypeStruct((width, hidden), BF),
+            jax.ShapeDtypeStruct((hidden, width), BF),
+            jax.ShapeDtypeStruct((tok_rows, width), BF),
+            jax.ShapeDtypeStruct((tok_rows, width), BF),
+            jax.ShapeDtypeStruct((2, tok_rows), jnp.float32),
         ],
-        in_specs=[whole(x), whole(dy), whole(mixed), whole(mixed), whole(grad_combine)]
-        + [pl.BlockSpec((1, take, 3, rows, CHUNK), lambda n: (n // steps, n % steps, 0, 0, 0))],
-        out_specs=[
-            pl.BlockSpec((1, width, take * CHUNK), lambda n: (0, 0, n)),
-            pl.BlockSpec((1, width, take * CHUNK), lambda n: (0, 0, n)),
-            pl.BlockSpec((1, take * CHUNK, width), lambda n: (0, n, 0)),
-            whole(mixed),
-            whole(mixed),
-            whole(grad_combine),
-        ],
-        name="weight_grads",
-        cost_estimate=pl.CostEstimate(
-            flops=6 * width * rows * hidden,
-            bytes_accessed=6 * hidden * (rows + width),
-            transcendentals=0,
-        ),
-    )(x, dy, mixed, grad_tokens, grad_combine, blocks)
+        in_specs=[whole] * 6,
+        out_specs=[any_place] * 6,
+        scratch_shapes=[pltpu.SemaphoreType.DMA((4, max(3, hidden // CHUNK)))],
+        compiler_params=pltpu.CompilerParams(vmem_limit_bytes=4 << 20),
+        name="place_results",
+    )(gate_buf, up_buf, down_buf, mixed, grad_tokens, grad_combine)
 
 
 def body(tokens, cotangent, expert_ids, combine_weights, w_gate, w_up, w_down):
@@ -904,13 +967,11 @@
         return general_body(tokens, cotangent, expert_ids, combine_weights, w_gate, w_up, w_down)
     tok_rows, chosen = expert_ids.shape
     capacity = tok_rows * chosen * 5 // (3 * lax.axis_size("ep"))
-    blocks, x, dy, mixed, grad_tokens, grad_combine = layer(
-        expert_ids, expert_ids.T, combine_weights, tokens, cotangent, w_gate[0], w_up[0], w_down[0], capacity
-    )
-    gate, up, down, mixed, grad_tokens, grad_combine = weight_grads(
-        x, dy, mixed, grad_tokens, grad_combine, blocks
-    )
-    return mixed, grad_tokens, grad_combine, gate, up, down
+    held = layer(
+        expert_ids.T, combine_weights.T, tokens, cotangent, w_gate[0], w_up[0], w_down[0], capacity
+    )
+    gate, up, down, mixed, grad_tokens, grad_combine = place_results(*held)
+    return mixed, grad_tokens, grad_combine.T, gate[None], up[None], down[None]
 
 
 def solution(mesh):

time: 149 us -> 113 us (0.76)
  Pallas kernels: 143 us -> 112 us
  local copies, waits for them, and re-layouts: 4.22 us -> 0 us
    pallas_call x1, Pallas kernels: 122 us -> 104 us  [layer(): pl.pallas_call(functools.partial(layer_kernel, chips, groups, capacity),...]
    pallas_call x1, Pallas kernels: 21.2 us -> 7.58 us  [place_results(): pl.pallas_call(place_kernel, out_shape=[jax.ShapeDtypeStruct((width, hidd...]
    unnamed x3 -> x0, local copies, waits for them, and re-layouts: 4.22 us -> none
where the time goes in v2:
time: 113 us
  Pallas kernels  112 us (99%)
    pallas_call x1, Pallas kernels, layer(): pl.pallas_call(functools.partial(layer_kernel, chips, groups, capacity),...  104 us
    pallas_call x1, Pallas kernels, place_results(): pl.pallas_call(place_kernel, out_shape=[jax.ShapeDtypeStruct((width, hidd...  7.58 us

profile of v2, /device:TPU:0, one launch (start us, length us, event | category | flops | bytes accessed | tf_op | source)
XLA Modules:
  0.0 112.5 jit_solution(18375995551506528508)
XLA Ops:
  0.6 104.3 %layer.1 = (bf16[12288,256]{1,0:T(8,128)(2,1)S(1)}, bf16[12288,256]{1,0:T(8,128)(2,1)S(1)}, bf16[4096,768]{1,0:T(8,128)(2,1)S(1)}, bf16[96,384]{1,0:T(8,128)(2,1...) custom-call(s32[2,96]{1,0:T(2,128)} %bitcast.12, f32[2,96]{1,0:T(2,128)} %bitcast.13, bf16[96,384]{1,0:T(8,128)(2,1)} %tokens.1, ...), custom_call_target="tpu_custom_call" | custom-call | tf_op jit(solution)/shard_map/layer/pallas_call | solution.py:871
  105.0 7.6 %place_results.1 = (bf16[384,8192]{1,0:T(8,128)(2,1)}, bf16[384,8192]{1,0:T(8,128)(2,1)}, bf16[8192,384]{1,0:T(8,128)(2,1)}, bf16[96,384]{1,0:T(8,128)(2,1)}, bf16[96,384]{1,0:T(8,128)(2,1)}, /*index=5*/f32[2,96]{1,0:T(2,128)}) custom-call(bf16[12288,256]{1,0:T(8,128)(2,1)S(1)} %get-tuple-element.18.gate_buf, ...), custom_call_target="tpu_custom_call" | custom-call | tf_op jit(solution)/shard_map/place_results/pallas_call | solution.py:947

commit v3 on v0

--- a/solution.py
+++ b/solution.py
@@ -260,7 +260,7 @@
     )
 
 
-def body(tokens, cotangent, expert_ids, combine_weights, w_gate, w_up, w_down):
+def general_body(tokens, cotangent, expert_ids, combine_weights, w_gate, w_up, w_down):
     groups = lax.axis_size("ep")
     tok_rows, piece_width = tokens.shape
     chosen = expert_ids.shape[1]
@@ -370,6 +370,664 @@
     )
 
 
+CHUNK = 256
+LANES = 128
+
+
+def fast_form(tokens, expert_ids, w_gate):
+    groups, size = lax.axis_size("ep"), lax.axis_size("tp")
+    tok_rows, width = tokens.shape
+    hidden = w_gate.shape[2]
+    capacity = tok_rows * expert_ids.shape[1] * 5 // (3 * groups)
+    return (
+        size == 8
+        and expert_ids.shape[1] == 2
+        and 3 <= groups <= 8
+        and width % LANES == 0
+        and hidden % CHUNK == 0
+        and capacity % 16 == 0
+        and capacity <= LANES
+        and groups * capacity % 32 == 0
+        and tok_rows <= LANES
+        and tok_rows % 16 == 0
+    )
+
+
+def far_copy(src, dst, send, recv, device):
+    return pltpu.make_async_remote_copy(
+        src_ref=src, dst_ref=dst, send_sem=send, recv_sem=recv, device_id=device, device_id_type=MESH
+    )
+
+
+def layer_kernel(
+    chips,
+    groups,
+    capacity,
+    ids_hbm,
+    weights_hbm,
+    tokens_hbm,
+    cotangent_hbm,
+    wg_hbm,
+    wu_hbm,
+    wd_hbm,
+    gate_buf,
+    up_buf,
+    down_buf,
+    mixed,
+    grad_tokens,
+    grad_combine,
+    blocks,
+    both,
+    out_rows,
+    factors,
+    part,
+    pre,
+    stage,
+    back,
+    ready,
+    got,
+    turned,
+    inner_sum,
+    inner_out,
+    inner_in,
+    products,
+    table,
+    ids_t,
+    weights_t,
+    tokens,
+    cotangent,
+    in_sem,
+    w_sem,
+    z_recv,
+    x_side,
+    x_far,
+    x_pass,
+    a_side,
+    a_far,
+    a_own,
+    a_pass,
+    s_recv,
+    recv,
+    send,
+):
+    size = 2 * chips
+    tok_rows, width = tokens.shape
+    rows = groups * capacity
+    model = size * width
+    hidden = wg_hbm.shape[1]
+    chunks = hidden // CHUNK
+    wide = 2 * width
+    order = ring_order(chips)
+    place = [order.index(chip) for chip in range(chips)]
+    me = lax.axis_index("tp")
+    group = lax.axis_index("ep")
+    chip, core = me // 2, me % 2
+    spot = pick(place, chip)
+    partner = chip * 2 + 1 - core
+
+    def at(offset):
+        return pick(order, (spot + offset + chips) % chips) * 2 + core
+
+    right, left, across = at(1), at(-1), at(2)
+    sides = (right, left)
+
+    def other(device):
+        return device // 2 * 2 + 1 - core
+
+    near = [sorted(range(groups), key=lambda s: (abs(s - g), s)) for g in range(groups)]
+    planes = [pick([near[g][k] for g in range(groups)], group) for k in range(groups)]
+
+    def rows_of(s):
+        return pl.ds(pl.multiple_of(s * capacity, 16), capacity)
+
+    def cols_of(device):
+        return pl.ds(pl.multiple_of(device * width, LANES), width)
+
+    def take(block, sem, device):
+        far_copy(block, block, send.at[0], sem, device).wait_recv()
+
+    barrier = pltpu.get_barrier_semaphore()
+    for k in range(1, groups):
+        pl.semaphore_signal(barrier, inc=1, device_id={"ep": planes[k]}, device_id_type=MESH)
+    for d in range(1, size):
+        pl.semaphore_signal(barrier, inc=1, device_id={"tp": (me + d) % size}, device_id_type=MESH)
+
+    inputs = (
+        (ids_hbm, ids_t),
+        (weights_hbm, weights_t),
+        (tokens_hbm, tokens),
+        (cotangent_hbm, cotangent),
+    )
+    inputs = [pltpu.make_async_copy(a, b, in_sem.at[n]) for n, (a, b) in enumerate(inputs)]
+    for copy in inputs:
+        copy.start()
+    for copy in inputs:
+        copy.wait()
+    row_id = lax.broadcasted_iota(jnp.int32, (8, tok_rows), 0)
+    member_t = jnp.where((ids_t[0:1, :] == row_id) | (ids_t[1:2, :] == row_id), 1.0, 0.0)
+    first = lax.broadcasted_iota(jnp.int32, (tok_rows, tok_rows), 0)
+    second = lax.broadcasted_iota(jnp.int32, (tok_rows, tok_rows), 1)
+    before_t = jnp.dot(
+        member_t.astype(BF),
+        jnp.where(first < second, 1.0, 0.0).astype(BF),
+        preferred_element_type=jnp.float32,
+    )
+    table[...] = jnp.zeros((LANES, LANES), jnp.float32)
+    table[0:2, 0:tok_rows] = ids_t[...].astype(jnp.float32)
+    table[2:4, 0:tok_rows] = weights_t[...]
+    columns = jnp.transpose(table[...])[0:tok_rows, :]
+    choice = (columns[:, 0:1], columns[:, 1:2])
+    weight = (columns[:, 2:3], columns[:, 3:4])
+    slot_t = lax.broadcasted_iota(jnp.int32, (capacity, tok_rows), 0).astype(jnp.float32)
+    for p in range(groups):
+        placer = (
+            jnp.where(slot_t == before_t[p : p + 1, :], 1.0, 0.0) * member_t[p : p + 1, :]
+        ).astype(BF)
+        own_weight = jnp.where(choice[0] == p, weight[0], 0.0) + jnp.where(choice[1] == p, weight[1], 0.0)
+        scaled = (own_weight * cotangent[...].astype(jnp.float32)).astype(BF)
+        out_rows[p, 0] = jnp.dot(placer, tokens[...], preferred_element_type=jnp.float32).astype(BF)
+        out_rows[p, 1] = jnp.dot(placer, scaled, preferred_element_type=jnp.float32).astype(BF)
+
+    pl.semaphore_wait(barrier, size + groups - 2)
+
+
+    def z_first(a):
+        for k in range(groups - 1, 0, -1):
+            far_copy(
+                out_rows.at[planes[k], a],
+                both.at[a, rows_of(group), cols_of(me)],
+                send.at[0],
+                z_recv.at[a, group],
+                {"ep": planes[k]},
+            ).start()
+
+    z_first(0)
+
+    def x_block(a, k, device):
+        return both.at[a, rows_of(planes[k]), cols_of(device)]
+
+    def x_send(a, k, device, sem, target):
+        block = x_block(a, k, device)
+        far_copy(block, block, send.at[1], sem, {"tp": target}).start()
+
+    def x_first(a, k):
+        if k == 0:
+            both[a, rows_of(group), cols_of(me)] = out_rows[group, a]
+        else:
+            take(x_block(a, k, me), z_recv.at[a, planes[k]], {"ep": planes[k]})
+        for way in range(2):
+            x_send(a, k, me, x_side.at[a, way, k], sides[way])
+        if a == 0 and k > 0:
+            x_send(a, k, me, x_far.at[a, k], across)
+        x_send(a, k, me, x_pass.at[a], partner)
+
+    def x_relay(a, k):
+        for way in range(2):
+            origin = sides[1 - way]
+            take(x_block(a, k, origin), x_side.at[a, way, k], {"tp": origin})
+            if (a + k) % 2 == way and (a == 1 or k == 0):
+                x_send(a, k, origin, x_far.at[a, k], sides[way])
+            x_send(a, k, origin, x_pass.at[a], partner)
+
+    def x_last(a, k):
+        take(x_block(a, k, across), x_far.at[a, k], {"tp": sides[1 - (a + k) % 2]})
+        x_send(a, k, across, x_pass.at[a], partner)
+
+    def x_whole(a):
+        take(both.at[a, :, pl.ds(0, chips * width)], x_pass.at[a], {"tp": partner})
+
+    def fetch(n):
+        source, target = ((wg_hbm, gate_buf), (wu_hbm, up_buf), (wd_hbm, down_buf))[n]
+        if n < 2:
+            for c in range(chunks):
+                pltpu.make_async_copy(
+                    source.at[:, pl.ds(c * CHUNK, CHUNK)],
+                    target.at[pl.ds(c * model, model), :],
+                    w_sem.at[n],
+                ).start()
+        else:
+            for q in range(chips):
+                pltpu.make_async_copy(
+                    source.at[:, pl.ds(q * wide, wide)],
+                    target.at[pl.ds(q * hidden, hidden), :],
+                    w_sem.at[n],
+                ).start()
+
+    def fetched(n):
+        target = (gate_buf, up_buf, down_buf)[n]
+        pltpu.make_async_copy(target, target, w_sem.at[n]).wait()
+
+    x_first(0, 0)
+    x_first(1, 0)
+    for n in range(3):
+        fetch(n)
+    x_relay(0, 0)
+    for k in range(1, groups):
+        x_first(0, k)
+        if k == 2:
+            z_first(1)
+        if k == 1:
+            x_relay(1, 0)
+            x_last(0, 0)
+        else:
+            x_relay(0, k - 1)
+        if k == groups - 1:
+            x_last(1, 0)
+    x_first(1, 1)
+    x_relay(0, groups - 1)
+    x_last(0, 1)
+    x_first(1, 2)
+    x_relay(1, 1)
+    for k in range(3, groups):
+        x_last(0, k - 1)
+        x_first(1, k)
+    x_last(0, groups - 1)
+    x_whole(0)
+    fetched(0)
+    fetched(1)
+
+    half = rows // 2
+    kinds = ((0, 1), (1, 2))
+
+    def a_block(b, c, device, way=None):
+        start, count = kinds[b]
+        if way is None:
+            return blocks.at[device, c, pl.ds(start, count)]
+        return blocks.at[device, c, pl.ds(start, count), pl.ds(way * half, half), :]
+
+    def a_send(b, c, device, sem, target, way=None):
+        block = a_block(b, c, device, way)
+        far_copy(block, block, send.at[2], sem, {"tp": target}).start()
+
+    def a_first(b, c):
+        for way in range(2):
+            a_send(b, c, me, a_side.at[b, way, c], sides[way])
+        a_send(b, c, me, a_own.at[b], partner)
+
+    def a_relay(b, c):
+        for way in range(2):
+            origin = sides[1 - way]
+            take(a_block(b, c, origin), a_side.at[b, way, c], {"tp": origin})
+            a_send(b, c, origin, a_far.at[b, c], sides[way], way)
+            a_send(b, c, origin, a_pass.at[b, 0, c], partner)
+
+    def a_relayed(b, c):
+        start, count = kinds[b]
+        take(blocks.at[pl.ds(0, 2), c, pl.ds(start, count)], a_pass.at[b, 0, c], {"tp": partner})
+
+    def a_last(b, c):
+        take(a_block(b, c, across), a_far.at[b, c], {"tp": left})
+        a_send(b, c, across, a_pass.at[b, 1, c], partner)
+
+    def a_lasted(b, c):
+        take(a_block(b, c, other(across)), a_pass.at[b, 1, c], {"tp": partner})
+
+    def hidden_chunk(c):
+        spread = pl.ds(c * model, model)
+        gate_pre = jnp.dot(both[0], gate_buf[spread, :], preferred_element_type=jnp.float32)
+        up_pre = jnp.dot(both[0], up_buf[spread, :], preferred_element_type=jnp.float32)
+        active, slope = silu_parts(gate_pre)
+        blocks[me, c, 0] = (active * up_pre).astype(BF)
+        factors[0, c] = up_pre * slope
+        factors[1, c] = active
+
+    later = [(x_last, k) for k in range(1, groups)]
+    split = [len(later) * c // max(1, chunks - 1) for c in range(chunks)]
+    done = 0
+    for c in range(chunks):
+        hidden_chunk(c)
+        if c == 0:
+            for k in range(2, groups):
+                x_relay(1, k)
+        a_first(0, c)
+        for step, k in later[done : split[c]]:
+            step(1, k)
+        done = split[c]
+    x_whole(1)
+    fetched(2)
+    inner_sum[...] = jnp.zeros((rows, LANES), jnp.float32)
+
+    def grad_chunk(c, _):
+        grad_hidden = None
+        for q in range(chips):
+            cut = pl.ds(pl.multiple_of(q * hidden + c * CHUNK, CHUNK), CHUNK)
+            term = contract_cols(both[1, :, q * wide : (q + 1) * wide], down_buf[cut, :])
+            grad_hidden = term if q == 0 else grad_hidden + term
+        blocks[me, c, 1] = (grad_hidden * factors[0, c]).astype(BF)
+        blocks[me, c, 2] = (grad_hidden * factors[1, c]).astype(BF)
+        a_first(1, c)
+        product = blocks[me, c, 0].astype(jnp.float32) * grad_hidden
+        total = inner_sum[...]
+        for n in range(CHUNK // LANES):
+            total = total + product[:, n * LANES : (n + 1) * LANES]
+        inner_sum[...] = total
+        return 0
+
+    lax.fori_loop(0, chunks, grad_chunk, 0)
+
+    turns = [2, 1, chips - 1, 0]
+
+    def swap(a, o, value):
+        part[a, 0, o] = value[:, :width].astype(BF)
+        part[a, 1, o] = value[:, width:].astype(BF)
+        far_copy(
+            part.at[a, 1 - core, o], pre.at[a, o], send.at[3], s_recv.at[a, o], {"tp": partner}
+        ).start()
+
+    def out_part(o, _):
+        q = pick(order, (spot + pick(turns, o)) % chips)
+        value = None
+        for c in range(chunks):
+            cut = pl.ds(pl.multiple_of(q * hidden + c * CHUNK, CHUNK), CHUNK)
+            term = jnp.dot(blocks[me, c, 0], down_buf[cut, :], preferred_element_type=jnp.float32)
+            value = term if c == 0 else value + term
+        swap(0, o, value)
+        return 0
+
+    def in_part(o, _):
+        q = pick(order, (spot + pick(turns, o)) % chips)
+        value = None
+        for c in range(chunks):
+            cut = pl.ds(pl.multiple_of(c * model + q * wide, LANES), wide)
+            term = contract_cols(blocks[me, c, 1], gate_buf[cut, :]) + contract_cols(
+                blocks[me, c, 2], up_buf[cut, :]
+            )
+            value = term if c == 0 else value + term
+        swap(1, o, value)
+        return 0
+
+    def spread_parts(a):
+        for o in range(chips):
+            take(pre.at[a, o], s_recv.at[a, o], {"tp": partner})
+
+            def add(s, _):
+                cut = rows_of(s)
+                stage[a, o, cut, :] = (
+                    part[a, core, o, cut, :].astype(jnp.float32) + pre[a, o, cut, :].astype(jnp.float32)
+                ).astype(BF)
+                return 0
+
+            lax.fori_loop(0, groups, add, 0)
+            for k in range(groups - 1, 0, -1):
+                far_copy(
+                    stage.at[a, o, rows_of(planes[k]), :],
+                    back.at[a, rows_of(group), pl.ds(o * width, width)],
+                    send.at[4],
+                    recv.at[0],
+                    {"ep": planes[k]},
+                ).start()
+            back[a, rows_of(group), o * width : (o + 1) * width] = stage[a, o, rows_of(group), :]
+
+    lax.fori_loop(0, chips, out_part, 0)
+    spread_parts(0)
+    lax.fori_loop(0, chips, in_part, 0)
+    spread_parts(1)
+
+    for p in range(groups):
+        value = inner_sum[p * capacity : (p + 1) * capacity, :]
+        if capacity < LANES:
+            value = jnp.concatenate(
+                [value, jnp.zeros((LANES - capacity, LANES), jnp.float32)], axis=0
+            )
+        value = jnp.sum(jnp.transpose(value), axis=0, keepdims=True)
+        inner_out[p] = jnp.broadcast_to(value, (8, LANES))
+    for k in range(1, groups):
+        far_copy(
+            inner_out.at[planes[k]], inner_in.at[group], send.at[5], recv.at[1], {"ep": planes[k]}
+        ).start()
+    inner_in[group] = inner_out[group]
+
+    turned[...] = jnp.transpose(both[0, :, cols_of(me)].astype(jnp.float32)).astype(BF)
+
+    def down_grads(device, c):
+        place_of = device * chunks + c
+        down_buf[
+            pl.ds(pl.multiple_of(place_of // 2 * CHUNK, CHUNK), CHUNK),
+            pl.ds(pl.multiple_of(place_of % 2 * width, LANES), width),
+        ] = contract_rows(blocks[device, c, 0], both[1, :, cols_of(me)]).astype(BF)
+
+    def side_grads(device, c):
+        spread = pl.ds(pl.multiple_of((device * chunks + c) * width, LANES), width)
+        gate_buf[spread, :] = jnp.dot(
+            turned[...], blocks[device, c, 1], preferred_element_type=jnp.float32
+        ).astype(BF)
+        up_buf[spread, :] = jnp.dot(
+            turned[...], blocks[device, c, 2], preferred_element_type=jnp.float32
+        ).astype(BF)
+
+    def grads_for(b, found):
+        devices, chunk = [d for d, _ in found], [c for _, c in found]
+
+        def step(n, _):
+            (down_grads, side_grads)[b](pick(devices, n), pick(chunk, n))
+            return 0
+
+        lax.fori_loop(0, len(found), step, 0)
+
+    def relays(b):
+        for c in range(chunks):
+            a_relay(b, c)
+            found = [(left, c), (right, c)]
+            if c > 0:
+                a_relayed(b, c - 1)
+                found += [(other(left), c - 1), (other(right), c - 1)]
+            grads_for(b, found)
+        a_relayed(b, chunks - 1)
+        grads_for(b, [(other(left), chunks - 1), (other(right), chunks - 1)])
+
+    for c in range(chunks):
+        a_relay(0, c)
+    take(blocks.at[partner, :, pl.ds(0, 1)], a_own.at[0], {"tp": partner})
+    take(blocks.at[partner, :, pl.ds(1, 2)], a_own.at[1], {"tp": partner})
+    for b in range(2):
+        grads_for(b, [(d, c) for c in range(chunks) for d in (me, partner)])
+    for c in range(chunks):
+        a_relayed(0, c)
+    grads_for(0, [(d, c) for c in range(chunks) for d in (left, right, other(left), other(right))])
+    relays(1)
+
+    take(inner_in.at[pl.ds(0, groups - 1)], recv.at[1], {"ep": planes[1]})
+    lane = lax.broadcasted_iota(jnp.int32, (tok_rows, LANES), 1)
+    lane_value = lane.astype(jnp.float32)
+    columns = jnp.transpose(table[...])[0:tok_rows, :]
+    choice = (columns[:, 0:1], columns[:, 1:2])
+    weight = (columns[:, 2:3], columns[:, 3:4])
+    member = jnp.where((choice[0] == lane_value) | (choice[1] == lane_value), 1.0, 0.0)
+    first = lax.broadcasted_iota(jnp.int32, (tok_rows, tok_rows), 0)
+    second = lax.broadcasted_iota(jnp.int32, (tok_rows, tok_rows), 1)
+    before = jnp.dot(
+        jnp.where(second < first, 1.0, 0.0).astype(BF),
+        member.astype(BF),
+        preferred_element_type=jnp.float32,
+    )
+    inner = jnp.zeros((tok_rows, LANES), jnp.float32)
+    takers = []
+    slot = lax.broadcasted_iota(jnp.int32, (tok_rows, rows), 1).astype(jnp.float32)
+    for k in range(2):
+        rank = jnp.sum(jnp.where(lane_value == choice[k], before, 0.0), axis=1, keepdims=True)
+        takers.append(jnp.where(slot == choice[k] * capacity + rank, 1.0, 0.0).astype(BF))
+        value = jnp.zeros((tok_rows, LANES), jnp.float32)
+        for p in range(groups):
+            value = value + jnp.where((lane_value == rank) & (choice[k] == p), inner_in[p][0:1, :], 0.0)
+        value = jnp.sum(value, axis=1, keepdims=True) / weight[k]
+        inner = inner + jnp.where(lane == k, value, 0.0)
+    if tok_rows < LANES:
+        inner = jnp.concatenate([inner, jnp.zeros((LANES - tok_rows, LANES), jnp.float32)], axis=0)
+    products[me] = jnp.transpose(inner)[0:8, :]
+    for d in range(1, size):
+        far_copy(
+            products.at[me], products.at[me], send.at[6], recv.at[2], {"tp": (me + d) % size}
+        ).start()
+
+    take(back.at[:, pl.ds(0, rows - capacity), :], recv.at[0], {"ep": planes[1]})
+    for n in range(chips // 2):
+        cut = slice(n * wide, (n + 1) * wide)
+        mix = weight[0] * jnp.dot(takers[0], back[0, :, cut], preferred_element_type=jnp.float32)
+        mix = mix + weight[1] * jnp.dot(
+            takers[1], back[0, :, cut], preferred_element_type=jnp.float32
+        )
+        grads = jnp.dot(takers[0] + takers[1], back[1, :, cut], preferred_element_type=jnp.float32)
+        for j in range(2):
+            o = 2 * n + j
+            ready[o, 0] = mix[:, j * width : (j + 1) * width].astype(BF)
+            ready[o, 1] = grads[:, j * width : (j + 1) * width].astype(BF)
+            if o < chips - 1:
+                far_copy(
+                    ready.at[o], got.at[o], send.at[7], recv.at[3], {"tp": at(turns[o])}
+                ).start()
+
+    for b in range(2):
+        for c in range(chunks):
+            a_last(b, c)
+            if c > 0:
+                a_lasted(b, c - 1)
+                grads_for(b, [(across, c), (other(across), c - 1)])
+            else:
+                grads_for(b, [(across, c)])
+        a_lasted(b, chunks - 1)
+        grads_for(b, [(other(across), chunks - 1)])
+
+    take(products.at[pl.ds(0, size - 1)], recv.at[2], {"tp": partner})
+    summed = products[0]
+    for d in range(1, size):
+        summed = summed + products[d]
+    grad_combine[...] = summed[0:2, 0:tok_rows]
+
+    take(got, recv.at[3], {"tp": right})
+    for a, out in ((0, mixed), (1, grad_tokens)):
+        value = ready[chips - 1, a].astype(jnp.float32)
+        for o in range(chips - 1):
+            value = value + got[o, a].astype(jnp.float32)
+        out[...] = value.astype(BF)
+
+    def sent(block, n):
+        far_copy(block, block, send.at[n], recv.at[0], {"tp": partner}).wait_send()
+
+    sent(out_rows.at[pl.ds(0, groups - 1)], 0)
+    sent(both.at[:, :, pl.ds(0, (chips + 3) * width)], 1)
+    sent(blocks.at[pl.ds(0, chips + 3)], 2)
+    sent(part.at[:, 0], 3)
+    sent(back.at[:, pl.ds(0, rows - capacity), :], 4)
+    sent(inner_out.at[pl.ds(0, groups - 1)], 5)
+    sent(products.at[pl.ds(0, size - 1)], 6)
+    sent(ready.at[pl.ds(0, chips - 1)], 7)
+
+
+def layer(ids_t, weights_t, tokens, cotangent, w_gate, w_up, w_down, capacity):
+    size, groups = lax.axis_size("tp"), lax.axis_size("ep")
+    chips = size // 2
+    tok_rows, width = tokens.shape
+    model, hidden = w_gate.shape
+    chunks = hidden // CHUNK
+    rows = groups * capacity
+    whole, any_place = pl.BlockSpec(memory_space=pltpu.VMEM), pl.BlockSpec(memory_space=pl.ANY)
+    dma = pltpu.SemaphoreType.DMA
+    return pl.pallas_call(
+        functools.partial(layer_kernel, chips, groups, capacity),
+        out_shape=[
+            pltpu.VMEM((chunks * model, CHUNK), BF),
+            pltpu.VMEM((chunks * model, CHUNK), BF),
+            pltpu.VMEM((chips * hidden, 2 * width), BF),
+            pltpu.VMEM((tok_rows, width), BF),
+            pltpu.VMEM((tok_rows, width), BF),
+            pltpu.VMEM((2, tok_rows), jnp.float32),
+        ],
+        in_specs=[any_place] * 7,
+        out_specs=[whole] * 6,
+        scratch_shapes=[
+            pltpu.VMEM((size, chunks, 3, rows, CHUNK), BF),
+            pltpu.VMEM((2, rows, model), BF),
+            pltpu.VMEM((groups, 2, capacity, width), BF),
+            pltpu.VMEM((2, chunks, rows, CHUNK), jnp.float32),
+            pltpu.VMEM((2, 2, chips, rows, width), BF),
+            pltpu.VMEM((2, chips, rows, width), BF),
+            pltpu.VMEM((2, chips, rows, width), BF),
+            pltpu.VMEM((2, rows, chips * width), BF),
+            pltpu.VMEM((chips, 2, tok_rows, width), BF),
+            pltpu.VMEM((chips - 1, 2, tok_rows, width), BF),
+            pltpu.VMEM((width, rows), BF),
+            pltpu.VMEM((rows, LANES), jnp.float32),
+            pltpu.VMEM((groups, 8, LANES), jnp.float32),
+            pltpu.VMEM((groups, 8, LANES), jnp.float32),
+            pltpu.VMEM((size, 8, LANES), jnp.float32),
+            pltpu.VMEM((LANES, LANES), jnp.float32),
+            pltpu.VMEM((2, tok_rows), jnp.int32),
+            pltpu.VMEM((2, tok_rows), jnp.float32),
+            pltpu.VMEM((tok_rows, width), BF),
+            pltpu.VMEM((tok_rows, width), BF),
+            dma((4,)),
+            dma((3,)),
+            dma((2, groups)),
+            dma((2, 2, groups)),
+            dma((2, groups)),
+            dma((2,)),
+            dma((2, 2, chunks)),
+            dma((2, chunks)),
+            dma((2,)),
+            dma((2, 2, chunks)),
+            dma((2, chips)),
+            dma((4,)),
+            dma((8,)),
+        ],
+        compiler_params=pltpu.CompilerParams(
+            collective_id=0, has_side_effects=True, vmem_limit_bytes=44 << 20
+        ),
+        name="layer",
+    )(ids_t, weights_t, tokens, cotangent, w_gate, w_up, w_down)
+
+
+def place_kernel(gate_buf, up_buf, down_buf, *refs):
+    small, (gate, up, down), outs, sems = refs[:3], refs[3:6], refs[6:9], refs[9]
+    width = gate.shape[0]
+    count = gate.shape[1] // CHUNK
+    for n in range(count):
+        cut, spread = pl.ds(n * CHUNK, CHUNK), pl.ds(n * width, width)
+        pltpu.make_async_copy(gate_buf.at[spread, :], gate.at[:, cut], sems.at[0]).start()
+        pltpu.make_async_copy(up_buf.at[spread, :], up.at[:, cut], sems.at[1]).start()
+        block = down_buf.at[pl.ds(n // 2 * CHUNK, CHUNK), pl.ds(n % 2 * width, width)]
+        pltpu.make_async_copy(block, down.at[cut, :], sems.at[2]).start()
+    for n in range(3):
+        pltpu.make_async_copy(small[n], outs[n], sems.at[3 + n]).start()
+    for n in range(3):
+        pltpu.make_async_copy(small[n], outs[n], sems.at[3 + n]).wait()
+    for n, result in enumerate((gate, up, down)):
+        pltpu.make_async_copy(result, result, sems.at[n]).wait()
+
+
+def place_results(gate_buf, up_buf, down_buf, mixed, grad_tokens, grad_combine):
+    tok_rows, width = mixed.shape
+    hidden = gate_buf.shape[0] // width * CHUNK
+    whole, any_place = pl.BlockSpec(memory_space=pltpu.VMEM), pl.BlockSpec(memory_space=pl.ANY)
+    return pl.pallas_call(
+        place_kernel,
+        out_shape=[
+            jax.ShapeDtypeStruct((width, hidden), BF),
+            jax.ShapeDtypeStruct((width, hidden), BF),
+            jax.ShapeDtypeStruct((hidden, width), BF),
+            jax.ShapeDtypeStruct((tok_rows, width), BF),
+            jax.ShapeDtypeStruct((tok_rows, width), BF),
+            jax.ShapeDtypeStruct((2, tok_rows), jnp.float32),
+        ],
+        in_specs=[whole] * 6,
+        out_specs=[any_place] * 6,
+        scratch_shapes=[pltpu.SemaphoreType.DMA((6,))],
+        compiler_params=pltpu.CompilerParams(vmem_limit_bytes=4 << 20),
+        name="place_results",
+    )(gate_buf, up_buf, down_buf, mixed, grad_tokens, grad_combine)
+
+
+def body(tokens, cotangent, expert_ids, combine_weights, w_gate, w_up, w_down):
+    if not fast_form(tokens, expert_ids, w_gate):
+        return general_body(tokens, cotangent, expert_ids, combine_weights, w_gate, w_up, w_down)
+    tok_rows, chosen = expert_ids.shape
+    capacity = tok_rows * chosen * 5 // (3 * lax.axis_size("ep"))
+    held = layer(
+        expert_ids.T, combine_weights.T, tokens, cotangent, w_gate[0], w_up[0], w_down[0], capacity
+    )
+    gate, up, down, mixed, grad_tokens, grad_combine = place_results(*held)
+    return mixed, grad_tokens, grad_combine.T, gate[None], up[None], down[None]
+
+
 def solution(mesh):
     placed = (
         P("ep", "tp"),

time: 261 us -> 106 us (0.41)
  matrix products: 37.1 us -> 0 us
  Pallas kernels: 139 us -> 105 us
  local copies, waits for them, and re-layouts: 24.5 us -> 0 us
  blocking collectives: 24.3 us -> 0 us
  starting transfers between devices: 18.1 us -> 0 us
  waiting for transfers between devices: 11.4 us -> 0 us
  other arithmetic: 4.56 us -> 0 us
    dot_general x9 -> x0, matrix products: 37.1 us -> none  [the longest x3 15 us: contract_cols(): lax.dot_general(left, right, (((1,), (1,)), ((), ())), preferred_element_...]
    pallas_call x5 -> x2, Pallas kernels: 139 us -> 105 us  [the longest x1 98.8 us: layer(): pl.pallas_call(functools.partial(layer_kernel, chips, groups, capacity),...]
    psum x1 -> x0, blocking collectives: 24.3 us -> none  [body(): grad_combine = lax.psum(local_products, 'tp')]
    all_to_all x4 -> x0, starting transfers between devices: 18.1 us -> none  [the longest x1 6.35 us: body(): lax.all_to_all(send_rows.reshape(groups, capacity, piece_width), 'ep', sp...]
    reshape x6 -> x0, local copies, waits for them, and re-layouts: 14.1 us -> none  [the longest x2 10.7 us: reduce_pieces(): p.reshape(rows, chips, 2, width).transpose(2, 1, 0, 3)]
    all_to_all x4 -> x0, waiting for transfers between devices: 11.4 us -> none  [the longest x1 5.98 us: body(): lax.all_to_all(send_grad.reshape(groups, capacity, piece_width), 'ep', sp...]
    unnamed x30 -> x0, local copies, waits for them, and re-layouts: 3.93 us -> none
  transfers between devices with their start and end apart: 4 -> 0, of which waited for: 2 -> 0; matrix products, arithmetic and copies ran while one was open for 6% -> 0% of each run, Pallas kernels for 34% -> 0%
where the time goes in v3:
time: 106 us
  Pallas kernels  105 us (99%)
    pallas_call x1, Pallas kernels, layer(): pl.pallas_call(functools.partial(layer_kernel, chips, groups, capacity),...  98.8 us
    pallas_call x1, Pallas kernels, place_results(): pl.pallas_call(place_kernel, out_shape=[jax.ShapeDtypeStruct((width, hidd...  6.49 us

profile of v3, /device:TPU:0, one launch (start us, length us, event | category | flops | bytes accessed | tf_op | source)
XLA Modules:
  0.0 106.1 jit_solution(2907050356444344139)
XLA Ops:
  0.6 98.8 %layer.1 = (bf16[12288,256]{1,0:T(8,128)(2,1)S(1)}, bf16[12288,256]{1,0:T(8,128)(2,1)S(1)}, bf16[4096,768]{1,0:T(8,128)(2,1)S(1)}, bf16[96,384]{1,0:T(8,128)(2,1...) custom-call(s32[2,96]{1,0:T(2,128)} %bitcast.12, f32[2,96]{1,0:T(2,128)} %bitcast.13, ...), custom_call_target="tpu_custom_call" | custom-call | tf_op jit(solution)/shard_map/layer/pallas_call | solution.py:925
  99.4 6.5 %place_results.1 = (bf16[384,8192]{1,0:T(8,128)(2,1)}, bf16[384,8192]{1,0:T(8,128)(2,1)}, bf16[8192,384]{1,0:T(8,128)(2,1)}, bf16[96,384]{1,0:T(8,128)(2,1)}, bf16[96,384]{1,0:T(8,128)(2,1)}, /*index=5*/f32[2,96]{1,0:T(2,128)}) custom-call(bf16[12288,256]{1,0:T(8,128)(2,1)S(1)} %get-tuple-element.18.gate_buf, ...), custom_call_target="tpu_custom_call" | custom-call | tf_op jit(solution)/shard_map/place_results/pallas_call | solution.py:1001

commit v4 on v3

--- a/solution.py
+++ b/solution.py
@@ -419,6 +419,8 @@
     blocks,
     both,
     out_rows,
+    dy_rows,
+    cots,
     factors,
     part,
     pre,
@@ -523,25 +525,22 @@
         placer = (
             jnp.where(slot_t == before_t[p : p + 1, :], 1.0, 0.0) * member_t[p : p + 1, :]
         ).astype(BF)
-        own_weight = jnp.where(choice[0] == p, weight[0], 0.0) + jnp.where(choice[1] == p, weight[1], 0.0)
-        scaled = (own_weight * cotangent[...].astype(jnp.float32)).astype(BF)
-        out_rows[p, 0] = jnp.dot(placer, tokens[...], preferred_element_type=jnp.float32).astype(BF)
-        out_rows[p, 1] = jnp.dot(placer, scaled, preferred_element_type=jnp.float32).astype(BF)
+        out_rows[p] = jnp.dot(placer, tokens[...], preferred_element_type=jnp.float32).astype(BF)
 
     pl.semaphore_wait(barrier, size + groups - 2)
 
 
-    def z_first(a):
-        for k in range(groups - 1, 0, -1):
-            far_copy(
-                out_rows.at[planes[k], a],
-                both.at[a, rows_of(group), cols_of(me)],
-                send.at[0],
-                z_recv.at[a, group],
-                {"ep": planes[k]},
-            ).start()
-
-    z_first(0)
+    for k in range(groups - 1, 0, -1):
+        far_copy(
+            out_rows.at[planes[k]],
+            both.at[0, rows_of(group), cols_of(me)],
+            send.at[0],
+            z_recv.at[0, group],
+            {"ep": planes[k]},
+        ).start()
+    for target in (across, right, left):
+        far_copy(cotangent, cots.at[chip], send.at[8], recv.at[4], {"tp": target}).start()
+    cots[chip] = cotangent[...]
 
     def x_block(a, k, device):
         return both.at[a, rows_of(planes[k]), cols_of(device)]
@@ -550,31 +549,72 @@
         block = x_block(a, k, device)
         far_copy(block, block, send.at[1], sem, {"tp": target}).start()
 
-    def x_first(a, k):
+    def side_of(k):
+        return 0 if k < 2 else 2
+
+    def x_first(k):
         if k == 0:
-            both[a, rows_of(group), cols_of(me)] = out_rows[group, a]
+            both[0, rows_of(group), cols_of(me)] = out_rows[group]
         else:
-            take(x_block(a, k, me), z_recv.at[a, planes[k]], {"ep": planes[k]})
+            take(x_block(0, k, me), z_recv.at[0, planes[k]], {"ep": planes[k]})
         for way in range(2):
-            x_send(a, k, me, x_side.at[a, way, k], sides[way])
-        if a == 0 and k > 0:
-            x_send(a, k, me, x_far.at[a, k], across)
-        x_send(a, k, me, x_pass.at[a], partner)
-
-    def x_relay(a, k):
+            x_send(0, k, me, x_side.at[way, k], sides[way])
+        if k > 0:
+            x_send(0, k, me, x_far.at[k], across)
+        x_send(0, k, me, x_pass.at[side_of(k)], partner)
+
+    def x_relay(k):
         for way in range(2):
             origin = sides[1 - way]
-            take(x_block(a, k, origin), x_side.at[a, way, k], {"tp": origin})
-            if (a + k) % 2 == way and (a == 1 or k == 0):
-                x_send(a, k, origin, x_far.at[a, k], sides[way])
-            x_send(a, k, origin, x_pass.at[a], partner)
-
-    def x_last(a, k):
-        take(x_block(a, k, across), x_far.at[a, k], {"tp": sides[1 - (a + k) % 2]})
-        x_send(a, k, across, x_pass.at[a], partner)
-
-    def x_whole(a):
-        take(both.at[a, :, pl.ds(0, chips * width)], x_pass.at[a], {"tp": partner})
+            take(x_block(0, k, origin), x_side.at[way, k], {"tp": origin})
+            if k == 0 and way == 0:
+                x_send(0, k, origin, x_far.at[k], sides[way])
+            x_send(0, k, origin, x_pass.at[side_of(k)], partner)
+
+    def x_last(k):
+        take(x_block(0, k, across), x_far.at[k], {"tp": across})
+        x_send(0, k, across, x_pass.at[side_of(k)], partner)
+
+    def dy_pass(k):
+        for q in range(chips):
+            x_send(1, k, q * 2 + core, x_pass.at[1], partner)
+
+    def dy_first():
+        take(cots.at[pl.ds(0, chips - 1)], recv.at[4], {"tp": across})
+        for p in range(groups):
+            placer = (
+                jnp.where(slot_t == before_t[p : p + 1, :], 1.0, 0.0) * member_t[p : p + 1, :]
+            ).astype(BF)
+            own_weight = jnp.where(choice[0] == p, weight[0], 0.0) + jnp.where(
+                choice[1] == p, weight[1], 0.0
+            )
+            for q in range(chips):
+                scaled = (own_weight * cots[q].astype(jnp.float32)).astype(BF)
+                dy_rows[p, q] = jnp.dot(placer, scaled, preferred_element_type=jnp.float32).astype(BF)
+        for k in range(1, groups):
+            for q in range(chips):
+                far_copy(
+                    dy_rows.at[planes[k], q],
+                    both.at[1, rows_of(group), cols_of(q * 2 + core)],
+                    send.at[9],
+                    z_recv.at[1, group],
+                    {"ep": planes[k]},
+                ).start()
+        for q in range(chips):
+            both[1, rows_of(group), cols_of(q * 2 + core)] = dy_rows[group, q]
+        dy_pass(0)
+
+    def dy_next(k):
+        take(
+            both.at[1, rows_of(planes[k]), pl.ds(0, chips * width)],
+            z_recv.at[1, planes[k]],
+            {"ep": planes[k]},
+        )
+        dy_pass(k)
+
+    def x_whole(a, n, count):
+        block = both.at[a, pl.ds(0, count * capacity), pl.ds(0, chips * width)]
+        take(block, x_pass.at[n], {"tp": partner})
 
     def fetch(n):
         source, target = ((wg_hbm, gate_buf), (wu_hbm, up_buf), (wd_hbm, down_buf))[n]
@@ -597,34 +637,21 @@
         target = (gate_buf, up_buf, down_buf)[n]
         pltpu.make_async_copy(target, target, w_sem.at[n]).wait()
 
-    x_first(0, 0)
-    x_first(1, 0)
+    x_first(0)
     for n in range(3):
         fetch(n)
-    x_relay(0, 0)
-    for k in range(1, groups):
-        x_first(0, k)
-        if k == 2:
-            z_first(1)
-        if k == 1:
-            x_relay(1, 0)
-            x_last(0, 0)
-        else:
-            x_relay(0, k - 1)
-        if k == groups - 1:
-            x_last(1, 0)
-    x_first(1, 1)
-    x_relay(0, groups - 1)
-    x_last(0, 1)
-    x_first(1, 2)
-    x_relay(1, 1)
+    x_relay(0)
+    x_first(1)
+    x_last(0)
+    x_first(2)
+    dy_first()
+    x_relay(1)
+    x_last(1)
     for k in range(3, groups):
-        x_last(0, k - 1)
-        x_first(1, k)
-    x_last(0, groups - 1)
-    x_whole(0)
-    fetched(0)
-    fetched(1)
+        x_first(k)
+    x_whole(0, 0, 2)
+    for n in range(3):
+        fetched(n)
 
     half = rows // 2
     kinds = ((0, 1), (1, 2))
@@ -662,29 +689,95 @@
     def a_lasted(b, c):
         take(a_block(b, c, other(across)), a_pass.at[b, 1, c], {"tp": partner})
 
-    def hidden_chunk(c):
+    def hidden_rows(c, k):
         spread = pl.ds(c * model, model)
-        gate_pre = jnp.dot(both[0], gate_buf[spread, :], preferred_element_type=jnp.float32)
-        up_pre = jnp.dot(both[0], up_buf[spread, :], preferred_element_type=jnp.float32)
+        cut = rows_of(planes[k])
+        held = both[0, cut, :]
+        gate_pre = jnp.dot(held, gate_buf[spread, :], preferred_element_type=jnp.float32)
+        up_pre = jnp.dot(held, up_buf[spread, :], preferred_element_type=jnp.float32)
         active, slope = silu_parts(gate_pre)
-        blocks[me, c, 0] = (active * up_pre).astype(BF)
-        factors[0, c] = up_pre * slope
-        factors[1, c] = active
-
-    later = [(x_last, k) for k in range(1, groups)]
-    split = [len(later) * c // max(1, chunks - 1) for c in range(chunks)]
+        blocks[me, c, 0, cut, :] = (active * up_pre).astype(BF)
+        block = blocks.at[me, c, pl.ds(0, 1), cut, :]
+        for way in range(2):
+            far_copy(block, block, send.at[2], a_side.at[0, way, c], {"tp": sides[way]}).start()
+        far_copy(block, block, send.at[2], a_own.at[0], {"tp": partner}).start()
+        factors[0, c, cut, :] = up_pre * slope
+        factors[1, c, cut, :] = active
+
+    turns = [2, 1, chips - 1, 0]
+
+    def swap(a, o, value):
+        part[a, 0, o] = value[:, :width].astype(BF)
+        part[a, 1, o] = value[:, width:].astype(BF)
+        far_copy(
+            part.at[a, 1 - core, o], pre.at[a, o], send.at[3], s_recv.at[a, o], {"tp": partner}
+        ).start()
+
+    def out_part(o, _):
+        q = pick(order, (spot + pick(turns, o)) % chips)
+        value = None
+        for c in range(chunks):
+            cut = pl.ds(pl.multiple_of(q * hidden + c * CHUNK, CHUNK), CHUNK)
+            term = jnp.dot(blocks[me, c, 0], down_buf[cut, :], preferred_element_type=jnp.float32)
+            value = term if c == 0 else value + term
+        swap(0, o, value)
+        return 0
+
+    def in_part(o, _):
+        q = pick(order, (spot + pick(turns, o)) % chips)
+        value = None
+        for c in range(chunks):
+            cut = pl.ds(pl.multiple_of(c * model + q * wide, LANES), wide)
+            term = contract_cols(blocks[me, c, 1], gate_buf[cut, :]) + contract_cols(
+                blocks[me, c, 2], up_buf[cut, :]
+            )
+            value = term if c == 0 else value + term
+        swap(1, o, value)
+        return 0
+
+    def spread_parts(a):
+        for o in range(chips):
+            take(pre.at[a, o], s_recv.at[a, o], {"tp": partner})
+
+            def add(s, _):
+                cut = rows_of(s)
+                stage[a, o, cut, :] = (
+                    part[a, core, o, cut, :].astype(jnp.float32) + pre[a, o, cut, :].astype(jnp.float32)
+                ).astype(BF)
+                return 0
+
+            lax.fori_loop(0, groups, add, 0)
+            for k in range(groups - 1, 0, -1):
+                far_copy(
+                    stage.at[a, o, rows_of(planes[k]), :],
+                    back.at[a, rows_of(group), pl.ds(o * width, width)],
+                    send.at[4],
+                    recv.at[0],
+                    {"ep": planes[k]},
+                ).start()
+            back[a, rows_of(group), o * width : (o + 1) * width] = stage[a, o, rows_of(group), :]
+
+    rest = [(x_relay, k) for k in range(2, groups)] + [(x_last, k) for k in range(2, groups)]
     done = 0
     for c in range(chunks):
-        hidden_chunk(c)
-        if c == 0:
-            for k in range(2, groups):
-                x_relay(1, k)
-        a_first(0, c)
-        for step, k in later[done : split[c]]:
-            step(1, k)
-        done = split[c]
-    x_whole(1)
-    fetched(2)
+        for k in range(2):
+            hidden_rows(c, k)
+        upto = len(rest) * (c + 1) // chunks
+        for step, k in rest[done:upto]:
+            step(k)
+        done = upto
+    x_whole(0, 2, groups - 2)
+    for c in range(chunks):
+        for k in range(2, groups):
+            hidden_rows(c, k)
+    lax.fori_loop(0, chips, out_part, 0)
+    a_relay(0, 0)
+    for k in range(1, groups):
+        if k < chunks - 1:
+            a_relay(0, k)
+        dy_next(k)
+    x_whole(1, 1, groups)
+    spread_parts(0)
     inner_sum[...] = jnp.zeros((rows, LANES), jnp.float32)
 
     def grad_chunk(c, _):
@@ -704,62 +797,9 @@
         return 0
 
     lax.fori_loop(0, chunks, grad_chunk, 0)
-
-    turns = [2, 1, chips - 1, 0]
-
-    def swap(a, o, value):
-        part[a, 0, o] = value[:, :width].astype(BF)
-        part[a, 1, o] = value[:, width:].astype(BF)
-        far_copy(
-            part.at[a, 1 - core, o], pre.at[a, o], send.at[3], s_recv.at[a, o], {"tp": partner}
-        ).start()
-
-    def out_part(o, _):
-        q = pick(order, (spot + pick(turns, o)) % chips)
-        value = None
-        for c in range(chunks):
-            cut = pl.ds(pl.multiple_of(q * hidden + c * CHUNK, CHUNK), CHUNK)
-            term = jnp.dot(blocks[me, c, 0], down_buf[cut, :], preferred_element_type=jnp.float32)
-            value = term if c == 0 else value + term
-        swap(0, o, value)
-        return 0
-
-    def in_part(o, _):
-        q = pick(order, (spot + pick(turns, o)) % chips)
-        value = None
-        for c in range(chunks):
-            cut = pl.ds(pl.multiple_of(c * model + q * wide, LANES), wide)
-            term = contract_cols(blocks[me, c, 1], gate_buf[cut, :]) + contract_cols(
-                blocks[me, c, 2], up_buf[cut, :]
-            )
-            value = term if c == 0 else value + term
-        swap(1, o, value)
-        return 0
-
-    def spread_parts(a):
-        for o in range(chips):
-            take(pre.at[a, o], s_recv.at[a, o], {"tp": partner})
-
-            def add(s, _):
-                cut = rows_of(s)
-                stage[a, o, cut, :] = (
-                    part[a, core, o, cut, :].astype(jnp.float32) + pre[a, o, cut, :].astype(jnp.float32)
-                ).astype(BF)
-                return 0
-
-            lax.fori_loop(0, groups, add, 0)
-            for k in range(groups - 1, 0, -1):
-                far_copy(
-                    stage.at[a, o, rows_of(planes[k]), :],
-                    back.at[a, rows_of(group), pl.ds(o * width, width)],
-                    send.at[4],
-                    recv.at[0],
-                    {"ep": planes[k]},
-                ).start()
-            back[a, rows_of(group), o * width : (o + 1) * width] = stage[a, o, rows_of(group), :]
-
-    lax.fori_loop(0, chips, out_part, 0)
-    spread_parts(0)
+    for c in range(max(1, min(groups, chunks - 1)), chunks):
+        a_relay(0, c)
+
     lax.fori_loop(0, chips, in_part, 0)
     spread_parts(1)
 
@@ -815,8 +855,6 @@
         a_relayed(b, chunks - 1)
         grads_for(b, [(other(left), chunks - 1), (other(right), chunks - 1)])
 
-    for c in range(chunks):
-        a_relay(0, c)
     take(blocks.at[partner, :, pl.ds(0, 1)], a_own.at[0], {"tp": partner})
     take(blocks.at[partner, :, pl.ds(1, 2)], a_own.at[1], {"tp": partner})
     for b in range(2):
@@ -904,7 +942,10 @@
         far_copy(block, block, send.at[n], recv.at[0], {"tp": partner}).wait_send()
 
     sent(out_rows.at[pl.ds(0, groups - 1)], 0)
-    sent(both.at[:, :, pl.ds(0, (chips + 3) * width)], 1)
+    sent(both.at[0, :, pl.ds(0, (chips + 3) * width)], 1)
+    sent(both.at[1, :, pl.ds(0, chips * width)], 1)
+    sent(cots.at[pl.ds(0, chips - 1)], 8)
+    sent(dy_rows.at[pl.ds(0, groups - 1)], 9)
     sent(blocks.at[pl.ds(0, chips + 3)], 2)
     sent(part.at[:, 0], 3)
     sent(back.at[:, pl.ds(0, rows - capacity), :], 4)
@@ -937,7 +978,9 @@
         scratch_shapes=[
             pltpu.VMEM((size, chunks, 3, rows, CHUNK), BF),
             pltpu.VMEM((2, rows, model), BF),
-            pltpu.VMEM((groups, 2, capacity, width), BF),
+            pltpu.VMEM((groups, capacity, width), BF),
+            pltpu.VMEM((groups, chips, capacity, width), BF),
+            pltpu.VMEM((chips, tok_rows, width), BF),
             pltpu.VMEM((2, chunks, rows, CHUNK), jnp.float32),
             pltpu.VMEM((2, 2, chips, rows, width), BF),
             pltpu.VMEM((2, chips, rows, width), BF),
@@ -958,16 +1001,16 @@
             dma((4,)),
             dma((3,)),
             dma((2, groups)),
-            dma((2, 2, groups)),
             dma((2, groups)),
-            dma((2,)),
+            dma((groups,)),
+            dma((3,)),
             dma((2, 2, chunks)),
             dma((2, chunks)),
             dma((2,)),
             dma((2, 2, chunks)),
             dma((2, chips)),
-            dma((4,)),
-            dma((8,)),
+            dma((5,)),
+            dma((10,)),
         ],
         compiler_params=pltpu.CompilerParams(
             collective_id=0, has_side_effects=True, vmem_limit_bytes=44 << 20

time: 106 us -> 102 us (0.962)
  Pallas kernels: 105 us -> 101 us
    pallas_call x1, Pallas kernels: 98.8 us -> 94.5 us  [layer(): pl.pallas_call(functools.partial(layer_kernel, chips, groups, capacity),...]
where the time goes in v4:
time: 102 us
  Pallas kernels  101 us (99%)
    pallas_call x1, Pallas kernels, layer(): pl.pallas_call(functools.partial(layer_kernel, chips, groups, capacity),...  94.5 us
    pallas_call x1, Pallas kernels, place_results(): pl.pallas_call(place_kernel, out_shape=[jax.ShapeDtypeStruct((width, hidd...  6.49 us

profile of v4, /device:TPU:0, one launch (start us, length us, event | category | flops | bytes accessed | tf_op | source)
XLA Modules:
  0.0 101.8 jit_solution(436869895908557087)
XLA Ops:
  0.6 94.5 %layer.1 = (bf16[12288,256]{1,0:T(8,128)(2,1)S(1)}, bf16[12288,256]{1,0:T(8,128)(2,1)S(1)}, bf16[4096,768]{1,0:T(8,128)(2,1)S(1)}, bf16[96,384]{1,0:T(8,128)(2,1...) custom-call(s32[2,96]{1,0:T(2,128)} %bitcast.12, f32[2,96]{1,0:T(2,128)} %bitcast.13, ...), custom_call_target="tpu_custom_call" | custom-call | tf_op jit(solution)/shard_map/layer/pallas_call | solution.py:966
  95.1 6.5 %place_results.1 = (bf16[384,8192]{1,0:T(8,128)(2,1)}, bf16[384,8192]{1,0:T(8,128)(2,1)}, bf16[8192,384]{1,0:T(8,128)(2,1)}, bf16[96,384]{1,0:T(8,128)(2,1)}, bf16[96,384]{1,0:T(8,128)(2,1)}, /*index=5*/f32[2,96]{1,0:T(2,128)}) custom-call(bf16[12288,256]{1,0:T(8,128)(2,1)S(1)} %get-tuple-element.18.gate_buf, ...), custom_call_target="tpu_custom_call" | custom-call | tf_op jit(solution)/shard_map/place_results/pallas_call | solution.py:1044

commit v5 on v4

--- a/solution.py
+++ b/solution.py
@@ -643,8 +643,8 @@
     x_relay(0)
     x_first(1)
     x_last(0)
+    dy_first()
     x_first(2)
-    dy_first()
     x_relay(1)
     x_last(1)
     for k in range(3, groups):
@@ -864,6 +864,21 @@
     grads_for(0, [(d, c) for c in range(chunks) for d in (left, right, other(left), other(right))])
     relays(1)
 
+    def across_grads(b, first, end):
+        for c in range(first, end):
+            a_last(b, c)
+            found = [(across, c)]
+            if c > 0:
+                a_lasted(b, c - 1)
+                found.append((other(across), c - 1))
+            grads_for(b, found)
+        if end == chunks:
+            a_lasted(b, chunks - 1)
+            grads_for(b, [(other(across), chunks - 1)])
+
+    across_grads(0, 0, chunks)
+    across_grads(1, 0, max(0, chunks - 2))
+
     take(inner_in.at[pl.ds(0, groups - 1)], recv.at[1], {"ep": planes[1]})
     lane = lax.broadcasted_iota(jnp.int32, (tok_rows, LANES), 1)
     lane_value = lane.astype(jnp.float32)
@@ -914,16 +929,7 @@
                     ready.at[o], got.at[o], send.at[7], recv.at[3], {"tp": at(turns[o])}
                 ).start()
 
-    for b in range(2):
-        for c in range(chunks):
-            a_last(b, c)
-            if c > 0:
-                a_lasted(b, c - 1)
-                grads_for(b, [(across, c), (other(across), c - 1)])
-            else:
-                grads_for(b, [(across, c)])
-        a_lasted(b, chunks - 1)
-        grads_for(b, [(other(across), chunks - 1)])
+    across_grads(1, max(0, chunks - 2), chunks)
 
     take(products.at[pl.ds(0, size - 1)], recv.at[2], {"tp": partner})
     summed = products[0]

time: 102 us -> 101 us (level)
  Pallas kernels: 101 us -> 99.7 us
    pallas_call x1, Pallas kernels: 94.5 us -> 93.2 us  [layer(): pl.pallas_call(functools.partial(layer_kernel, chips, groups, capacity),...]
where the time goes in v5:
time: 101 us
  Pallas kernels  99.7 us (99%)
    pallas_call x1, Pallas kernels, layer(): pl.pallas_call(functools.partial(layer_kernel, chips, groups, capacity),...  93.2 us
    pallas_call x1, Pallas kernels, place_results(): pl.pallas_call(place_kernel, out_shape=[jax.ShapeDtypeStruct((width, hidd...  6.49 us

profile of v5, /device:TPU:0, one launch (start us, length us, event | category | flops | bytes accessed | tf_op | source)
XLA Modules:
  0.0 100.5 jit_solution(6732520386851768317)
XLA Ops:
  0.6 93.2 %layer.1 = (bf16[12288,256]{1,0:T(8,128)(2,1)S(1)}, bf16[12288,256]{1,0:T(8,128)(2,1)S(1)}, bf16[4096,768]{1,0:T(8,128)(2,1)S(1)}, bf16[96,384]{1,0:T(8,128)(2,1...) custom-call(s32[2,96]{1,0:T(2,128)} %bitcast.12, f32[2,96]{1,0:T(2,128)} %bitcast.13, ...), custom_call_target="tpu_custom_call" | custom-call | tf_op jit(solution)/shard_map/layer/pallas_call | solution.py:972
  93.9 6.5 %place_results.1 = (bf16[384,8192]{1,0:T(8,128)(2,1)}, bf16[384,8192]{1,0:T(8,128)(2,1)}, bf16[8192,384]{1,0:T(8,128)(2,1)}, bf16[96,384]{1,0:T(8,128)(2,1)}, bf16[96,384]{1,0:T(8,128)(2,1)}, /*index=5*/f32[2,96]{1,0:T(2,128)}) custom-call(bf16[12288,256]{1,0:T(8,128)(2,1)S(1)} %get-tuple-element.18.gate_buf, ...), custom_call_target="tpu_custom_call" | custom-call | tf_op jit(solution)/shard_map/place_results/pallas_call | solution.py:1050
